TPU v7x, 32 devices: a whole 2x2x4 slice. The times are simulated.
32 devices in a mesh: ga: 16 (over z, y, x), band: 2 (over core).
Axes of the slice: x: 2, y: 2, z: 4, core: 2. Of those that a mesh axis runs over, the one named last changes fastest.
Arguments:
- psi: bfloat16 [65536, 2048], P('ga', 'band'), may hold values from -1 to 1
- trial: bfloat16 [65536, 256], P('ga', 'band'), may hold values from -1.25 to 1.25
- beta: bfloat16 [65536, 1536], P('ga'), may hold values from -0.0625 to 0.0625
- q_blocks: float32 [128, 18, 18], replicated, may hold values from -6 to 6
- atom_counts: int32 [128], replicated, may hold values from 1 to 18, 1536 in all
Outputs:
- intersection: float32 [2048, 256], P('band', 'ga')
Inputs may be any that keep to these rules, and one draw needn't show every extreme that they name: `atom_counts`: the counts sum to 1536; atoms own consecutive projectors in order, and some atom has exactly 18.
All inputs are finite; a program needn't handle non-finite values.
Results may differ from a plain program's by a relative error of at most 0.0003.
Values may be sent and summed in bfloat16 or wider, within the bound.
A program may use at most 64 MiB of HBM per device.

v0:
```python
import functools

import jax
import jax.numpy as jnp
from jax import lax
from jax.experimental import pallas as pl
from jax.experimental.pallas import tpu as pltpu
from jax.sharding import PartitionSpec as P

MESH = pl.DeviceIdType.MESH
precise = lax.Precision.HIGHEST
F32, BF16 = jnp.float32, jnp.bfloat16


def contract(left, right, precision=None):
    return lax.dot_general(
        left, right, (((0,), (0,)), ((), ())), precision=precision, preferred_element_type=F32
    )


def split2(x):
    hi = x.astype(BF16)
    return hi, (x - hi.astype(F32)).astype(BF16)


def kernel(
    n, inner, maxp, psi_h, trial_h, beta_h, q_ref, cnt_ref, out_ref,
    psi_v, beta_v, trial_v, trial_t, q_parts, qd, proj, in1, mid1, end1, wall, whl, s_buf,
    fin, in3, mid3, end3, trial_sem, beta_sem, psi_sem, send1, recv1, send1b, recv1b,
    send2, recv2, send2b, recv2b, xs, xr, send3, recv3, send3b, recv3b,
):
    me = lax.axis_index("ga")
    band = lax.axis_index("band")
    outer = n // inner
    w, z = lax.rem(me, inner), lax.div(me, inner)

    def mate(d):
        return lax.rem(w + d, inner)

    def far(e):
        return lax.rem(z + e, outer)

    def reach(to_z, to_w):
        return dict(device_id=(to_z * inner + to_w, band), device_id_type=MESH)

    g, cols = trial_v.shape
    p_size = beta_v.shape[1]
    nbands = psi_v.shape[1]
    natom = cnt_ref.shape[1]
    mp = q_ref.shape[0] // maxp
    r1 = cols // n
    r2 = out_ref.shape[0]
    beta_chunks = beta_sem.shape[0]
    bw = p_size // beta_chunks
    psi_chunks = psi_sem.shape[0]
    pw = nbands // psi_chunks
    s_chunks = xs.shape[0]
    sw = g // s_chunks

    def aligned(i, size):
        return pl.ds(i * size if isinstance(i, int) else pl.multiple_of(i * size, size), size)

    def beta_copy(c):
        at = (slice(None), pl.ds(c * bw, bw))
        return pltpu.make_async_copy(beta_h.at[at], beta_v.at[at], beta_sem.at[c])

    def psi_copy(c):
        at = (slice(None), pl.ds(c * pw, pw))
        return pltpu.make_async_copy(psi_h.at[at], psi_v.at[at], psi_sem.at[c])

    trial_copy = pltpu.make_async_copy(trial_h, trial_v, trial_sem)
    trial_copy.start()
    for c in range(beta_chunks):
        beta_copy(c).start()
    for c in range(psi_chunks):
        psi_copy(c).start()

    barrier = pltpu.get_barrier_semaphore()

    for d in range(1, inner):
        pl.semaphore_signal(barrier, inc=1, **reach(z, mate(d)))
    for e in range(1, outer):
        pl.semaphore_signal(barrier, inc=1, **reach(far(e), w))
    pl.semaphore_signal(barrier, inc=1, device_id=(me, 1 - band), device_id_type=MESH)

    cnt = cnt_ref[...].astype(F32)
    row = lax.broadcasted_iota(jnp.int32, (natom, natom), 0)
    col = lax.broadcasted_iota(jnp.int32, (natom, natom), 1)
    offs = jnp.sum(jnp.where(col < row, cnt, 0.0), axis=1, keepdims=True)
    own = jnp.sum(jnp.where(col == row, cnt, 0.0), axis=1, keepdims=True)
    q = q_ref[...]
    q_hi = q.astype(BF16)
    rest = q - q_hi.astype(F32)
    q_mid = rest.astype(BF16)
    q_parts[0] = q_hi
    q_parts[1] = q_mid
    q_parts[2] = (rest - q_mid.astype(F32)).astype(BF16)
    lanes = 256
    nd = qd.shape[0]

    def diagonals(c, _):
        ids = (c * lanes + lax.broadcasted_iota(jnp.int32, (natom, lanes), 1)).astype(F32)
        owns = (offs <= ids) & (ids < offs + own)
        pos = jnp.sum(jnp.where(owns, ids - offs, 0.0), axis=0, keepdims=True)
        count = jnp.sum(jnp.where(owns, jnp.broadcast_to(own, owns.shape), 0.0), axis=0, keepdims=True)
        pick = jnp.where(owns, 1.0, 0.0).astype(BF16)
        flat = jnp.dot(q_parts[0], pick, preferred_element_type=F32)
        flat += jnp.dot(q_parts[1], pick, preferred_element_type=F32)
        flat += jnp.dot(q_parts[2], pick, preferred_element_type=F32)
        q_row = jnp.zeros((mp, lanes), F32)
        for i in range(maxp):
            q_row += jnp.where(pos == float(i), flat[i * mp : (i + 1) * mp], 0.0)
        at = pos + lax.broadcasted_iota(jnp.int32, (nd, lanes), 0).astype(F32) - float(maxp - 1)
        entries = jnp.zeros((nd, lanes), F32)
        for j in range(maxp):
            entries += jnp.where(at == float(j), q_row[j : j + 1], 0.0)
        qd[:, aligned(c, lanes)] = jnp.where(at < count, entries, 0.0)
        return 0

    lax.fori_loop(0, p_size // lanes, diagonals, 0)

    trial_copy.wait()

    def turn(k, _):
        trial_t[:, aligned(k, sw)] = trial_v[aligned(k, sw), :].T
        return 0

    lax.fori_loop(0, s_chunks, turn, 0)

    pl.semaphore_wait(barrier, inner + outer - 1)

    def inner1(c, d):
        at = pl.ds(c * bw, bw)
        return pltpu.make_async_remote_copy(
            src_ref=proj.at[aligned(mate(d), outer * r1), at],
            dst_ref=in1.at[d, :, at],
            send_sem=send1.at[c, d],
            recv_sem=recv1.at[c, d],
            **reach(z, mate(d)),
        )

    def outer1(c, e):
        at = pl.ds(c * bw, bw)
        return pltpu.make_async_remote_copy(
            src_ref=mid1.at[aligned(far(e), r1), at],
            dst_ref=end1.at[e, :, at],
            send_sem=send1b.at[c, e],
            recv_sem=recv1b.at[c, e],
            **reach(far(e), w),
        )

    def middle1(c):
        at = pl.ds(c * bw, bw)
        total = proj[aligned(w, outer * r1), at]
        for d in range(1, inner):
            inner1(c, d).wait()
            total += in1[d, :, at]
        mid1[:, at] = total
        for e in range(1, outer):
            outer1(c, e).start()

    for c in range(beta_chunks):
        beta_copy(c).wait()
        at = pl.ds(c * bw, bw)
        proj[:, at] = jnp.dot(trial_t[...], beta_v[:, at], preferred_element_type=F32)
        for d in range(1, inner):
            inner1(c, d).start()
        if c:
            middle1(c - 1)
    middle1(beta_chunks - 1)

    for c in range(beta_chunks):
        for e in range(1, outer):
            outer1(c, e).wait()
    x = mid1[aligned(z, r1), :]
    for e in range(1, outer):
        x += end1[e]
    acc = jnp.zeros_like(x)
    for d in range(2 * maxp - 1):
        shift = (maxp - 1 - d) % p_size
        moved = x if shift == 0 else pltpu.roll(x, shift, axis=1)
        acc += qd[d : d + 1, :] * moved
    mine = w * outer + z
    wall[aligned(mine, r1), :] = acc

    def outer2(e):
        return pltpu.make_async_remote_copy(
            src_ref=wall.at[aligned(mine, r1), :],
            dst_ref=wall.at[aligned(mine, r1), :],
            send_sem=send2.at[e],
            recv_sem=recv2.at[e],
            **reach(far(e), w),
        )

    def inner2(e, d):
        block = w * outer + lax.rem(z + outer - e, outer)
        return pltpu.make_async_remote_copy(
            src_ref=wall.at[aligned(block, r1), :],
            dst_ref=wall.at[aligned(block, r1), :],
            send_sem=send2b.at[e, d],
            recv_sem=recv2b.at[e, d],
            **reach(z, mate(d)),
        )

    for e in range(1, outer):
        outer2(e).start()
    for e in range(outer):
        if e:
            outer2(e).wait()
        for d in range(1, inner):
            inner2(e, d).start()
    for e in range(outer):
        for d in range(1, inner):
            inner2(e, d).wait()
    hi, lo = split2(wall[...])
    whl[:cols, :] = hi
    whl[cols:, :] = lo

    base = band * (2 * cols)

    def exchange(k):
        at = (pl.ds(pl.multiple_of(base, 2 * cols), 2 * cols), aligned(k, sw))
        return pltpu.make_async_remote_copy(
            src_ref=s_buf.at[at],
            dst_ref=s_buf.at[at],
            send_sem=xs.at[k],
            recv_sem=xr.at[k],
            device_id=(me, 1 - band),
            device_id_type=MESH,
        )

    def lift(k, _):
        both = lax.dot_general(
            whl[...], beta_v[aligned(k, sw), :], (((1,), (1,)), ((), ())), preferred_element_type=F32
        )
        s = both[:cols] + both[cols:] + trial_t[:, aligned(k, sw)].astype(F32)
        s_hi, s_lo = split2(s)
        s_buf[pl.ds(pl.multiple_of(base, 2 * cols), cols), aligned(k, sw)] = s_hi
        s_buf[pl.ds(pl.multiple_of(base + cols, cols), cols), aligned(k, sw)] = s_lo
        exchange(k).start()
        return 0

    lax.fori_loop(0, s_chunks, lift, 0)

    def wait_x(k, _):
        exchange(k).wait()
        return 0

    lax.fori_loop(0, s_chunks, wait_x, 0)

    def inner3(c, d):
        return pltpu.make_async_remote_copy(
            src_ref=fin.at[:, mate(d), :, aligned(c, pw)],
            dst_ref=in3.at[d, :, :, aligned(c, pw)],
            send_sem=send3.at[c, d],
            recv_sem=recv3.at[c, d],
            **reach(z, mate(d)),
        )

    def outer3(c, e):
        return pltpu.make_async_remote_copy(
            src_ref=mid3.at[far(e), :, aligned(c, pw)],
            dst_ref=end3.at[e, :, aligned(c, pw)],
            send_sem=send3b.at[c, e],
            recv_sem=recv3b.at[c, e],
            **reach(far(e), w),
        )

    def middle3(c):
        for d in range(1, inner):
            inner3(c, d).wait()
        for to in range(outer):
            total = fin[to, w, :, aligned(c, pw)]
            for d in range(1, inner):
                total += in3[d, to, :, aligned(c, pw)]
            mid3[to, :, aligned(c, pw)] = total
        for e in range(1, outer):
            outer3(c, e).start()

    for c in range(psi_chunks):
        psi_copy(c).wait()

    def share(c):
        f = jnp.dot(s_buf[...], psi_v[:, aligned(c, pw)], preferred_element_type=F32)
        for b in range(2):
            at = 2 * b * cols
            whole = f[at : at + cols] + f[at + cols : at + 2 * cols]
            fin[b * half : (b + 1) * half, :, :, aligned(c, pw)] = whole.reshape(
                half, inner, r2, pw
            )
        for d in range(1, inner):
            inner3(c, d).start()

    half = outer // 2
    for c in range(psi_chunks):
        share(c)
        if c:
            middle3(c - 1)
    middle3(psi_chunks - 1)

    for c in range(psi_chunks):
        total = mid3[z, :, aligned(c, pw)]
        for e in range(1, outer):
            outer3(c, e).wait()
            total += end3[e, :, aligned(c, pw)]
        out_ref[:, aligned(c, pw)] = total


def fused(n, inner, blk, psi, trial, beta, q_blocks, atom_counts):
    g, cols = trial.shape
    nbands = psi.shape[1]
    p_size = beta.shape[1]
    natom, maxp = q_blocks.shape[:2]
    mp = -(-maxp // 8) * 8
    nd = -(-(2 * maxp - 1) // 8) * 8
    r1, r2 = cols // n, blk // n
    outer = n // inner
    beta_chunks, psi_chunks, s_chunks = 3, 4, 8
    q_flat = jnp.pad(q_blocks, ((0, 0), (0, 0), (0, mp - maxp)))
    q_flat = q_flat.transpose(1, 2, 0).reshape(maxp * mp, natom)
    dma = pltpu.SemaphoreType.DMA
    out = pl.pallas_call(
        functools.partial(kernel, n, inner, maxp),
        out_shape=jax.ShapeDtypeStruct((r2, nbands), F32),
        in_specs=[pl.BlockSpec(memory_space=pl.ANY)] * 3
        + [pl.BlockSpec(memory_space=pltpu.VMEM)] * 2,
        out_specs=pl.BlockSpec(memory_space=pltpu.VMEM),
        scratch_shapes=[
            pltpu.VMEM((g, nbands), BF16),
            pltpu.VMEM((g, p_size), BF16),
            pltpu.VMEM((g, cols), BF16),
            pltpu.VMEM((cols, g), BF16),
            pltpu.VMEM((3, maxp * mp, natom), BF16),
            pltpu.VMEM((nd, p_size), F32),
            pltpu.VMEM((cols, p_size), F32),
            pltpu.VMEM((inner, outer * r1, p_size), F32),
            pltpu.VMEM((outer * r1, p_size), F32),
            pltpu.VMEM((outer, r1, p_size), F32),
            pltpu.VMEM((cols, p_size), F32),
            pltpu.VMEM((2 * cols, p_size), BF16),
            pltpu.VMEM((4 * cols, g), BF16),
            pltpu.VMEM((outer, inner, r2, nbands), F32),
            pltpu.VMEM((inner, outer, r2, nbands), F32),
            pltpu.VMEM((outer, r2, nbands), F32),
            pltpu.VMEM((outer, r2, nbands), F32),
            dma,
            dma((beta_chunks,)),
            dma((psi_chunks,)),
            dma((beta_chunks, inner)),
            dma((beta_chunks, inner)),
            dma((beta_chunks, outer)),
            dma((beta_chunks, outer)),
            dma((outer,)),
            dma((outer,)),
            dma((outer, inner)),
            dma((outer, inner)),
            dma((s_chunks,)),
            dma((s_chunks,)),
            dma((psi_chunks, inner)),
            dma((psi_chunks, inner)),
            dma((psi_chunks, outer)),
            dma((psi_chunks, outer)),
        ],
        compiler_params=pltpu.CompilerParams(
            collective_id=0, has_side_effects=True, vmem_limit_bytes=60 * 1024 * 1024
        ),
    )(psi, trial, beta, q_flat, atom_counts.reshape(1, natom))
    return out.T


def q_dense(atom_counts, q_blocks, p_size):
    offsets = jnp.cumsum(atom_counts, dtype=jnp.int32) - atom_counts
    natom, maxp = q_blocks.shape[:2]
    ids = jnp.arange(p_size, dtype=jnp.int32)
    owns = (offsets[None, :] <= ids[:, None]) & (ids[:, None] < (offsets + atom_counts)[None, :])
    pos = jnp.sum(jnp.where(owns, ids[:, None] - offsets[None, :], 0), axis=1)
    atom = jnp.sum(jnp.where(owns, jnp.arange(natom, dtype=jnp.int32)[None, :], 0), axis=1)
    flat = jnp.dot(owns.astype(F32), q_blocks.reshape(natom, maxp * maxp), precision=precise)
    place = pos[:, None] == jnp.arange(maxp, dtype=jnp.int32)[None, :]
    rows = jnp.sum(jnp.where(place[:, :, None], flat.reshape(p_size, maxp, maxp), 0.0), axis=1)
    entries = jnp.dot(rows, place.astype(F32).T, precision=precise)
    return jnp.where(atom[:, None] == atom[None, :], entries, 0.0)


def general(psi, trial, beta, q_blocks, atom_counts):
    own = lax.psum(contract(beta, trial), "ga")
    weighted = jnp.dot(q_dense(atom_counts, q_blocks, beta.shape[1]), own, precision=precise)
    w_hi, w_lo = split2(weighted)
    both = jnp.dot(beta, jnp.concatenate([w_hi, w_lo], axis=1), preferred_element_type=F32)
    cols = trial.shape[1]
    s = both[:, :cols] + both[:, cols:] + trial.astype(F32)
    s_hi, s_lo = split2(lax.all_gather(s, "band", axis=1, tiled=True))
    part = contract(psi, s_hi) + contract(psi, s_lo)
    return lax.psum_scatter(part, "ga", scatter_dimension=1, tiled=True)


def solution(mesh):
    n, bands = mesh.shape["ga"], mesh.shape["band"]
    inner = 4

    def shards(psi, trial, beta, q_blocks, atom_counts):
        g, cols = trial.shape
        blk = cols * bands
        fits = (
            bands == 2
            and n % (2 * inner) == 0
            and cols % 128 == 0
            and cols % (8 * n) == 0
            and blk % (8 * n) == 0
            and g % 4096 == 0
            and beta.shape[1] % 768 == 0
            and psi.shape[1] % 512 == 0
            and q_blocks.shape[0] % 128 == 0
        )
        if fits:
            return fused(n, inner, blk, psi, trial, beta, q_blocks, atom_counts)
        return general(psi, trial, beta, q_blocks, atom_counts)

    in_specs = (P("ga", "band"), P("ga", "band"), P("ga", None), P(), P())
    out_specs = P("band", "ga")
    return jax.shard_map(shards, mesh=mesh, in_specs=in_specs, out_specs=out_specs, check_vma=False)
```

profile of v0, /device:TPU:0, one launch (start us, length us, event | category | flops | bytes accessed | tf_op | source)
XLA Modules:
  0.0 68.3 jit_solution(14598278654948082579)
XLA Ops:
  0.0 1.6 %pad.4 = f32[128,18,24]{0,2,1:T(8,128)} pad(f32[128,18,18]{0,2,1:T(8,128)} %param.8, f32[]{:T(128)} %constant.2.clone.1), padding=0_0x0_0x0_6 | pad | bytes 387076 | tf_op jit(solution)/shard_map/jit(_pad)/pad | solution.py:319
  1.6 65.2 %shard_map.55 = f32[16,1024]{1,0:T(8,128)} custom-call(bf16[4096,1024]{1,0:T(8,128)(2,1)} %psi_h.1, bf16[4096,128]{1,0:T(8,128)(2,1)} %trial_h.1, bf16[4096,1536]{1,0:T(8,128)(2,1)} %beta_h.1, f32[432,128]{1,0:T(8,128)} %bitcast.5, s32[1,128]{1,0:T(1,128)} %bitcast.7), custom_call_target="tpu_custom_call" | custom-call | tf_op jit(solution)/shard_map/pallas_call | solution.py:322
  66.8 1.5 %copy.7 = f32[1024,16]{0,1:T(8,128)} copy(f32[1024,16]{0,1:T(8,128)} %bitcast.6) | data formatting | bytes 131072
where the time goes:
time: 68.5 us; the launch traced here: 68.3 us
  Pallas kernels  65.2 us (95%)
  local copies, waits for them, and re-layouts  3.1 us (5%)
    pallas_call x1, Pallas kernels, fused(): pl.pallas_call(functools.partial(kernel, n, inner, maxp), out_shape=jax.S...  65.2 us
    pad x1, local copies, waits for them, and re-layouts, fused(): q_flat = jnp.pad(q_blocks, ((0, 0), (0, 0), (0, mp - maxp)))  1.62 us
    unnamed x1, local copies, waits for them, and re-layouts  1.47 us

commit v1 on v0

v1 whole, which is shorter than its diff:
```python
import functools

import jax
import jax.numpy as jnp
from jax import lax
from jax.experimental import pallas as pl
from jax.experimental.pallas import tpu as pltpu
from jax.sharding import PartitionSpec as P

MESH = pl.DeviceIdType.MESH
precise = lax.Precision.HIGHEST
F32, BF16, I16 = jnp.float32, jnp.bfloat16, jnp.int16
LEVELS, TINY = 32767.0, 1e-30


def contract(left, right, precision=None):
    return lax.dot_general(
        left, right, (((0,), (0,)), ((), ())), precision=precision, preferred_element_type=F32
    )


def split2(x):
    hi = x.astype(BF16)
    return hi, (x - hi.astype(F32)).astype(BF16)


def encode(x):
    top = jnp.maximum(jnp.max(jnp.abs(x), keepdims=True), TINY)
    return jnp.round(x * (LEVELS / top)).astype(jnp.int32).astype(I16), top * (1.0 / LEVELS)


def decode(code, scale):
    return code.astype(jnp.int32).astype(F32) * scale


def kernel(
    n, inner, maxp, psi_h, trial_h, beta_h, q_ref, cnt_ref, out_ref,
    psi_v, beta_v, trial_v, beta_t, trial_t, q_parts, qd, g_hi, g_lo, w_hi, w_lo,
    proj, code1, scale1, in1, in1s, mid1, code1b, scale1b, end1, end1s,
    wall, walls, fin, code3, scale3, in3, in3s, mid3, code3b, scale3b, end3, end3s,
    trial_sem, beta_sem, psi_sem, xs, xr,
    send1, recv1, send1b, recv1b, send2, recv2, send2b, recv2b, send2c, recv2c,
    send3, recv3, send3b, recv3b,
):
    me = lax.axis_index("ga")
    band = lax.axis_index("band")
    outer = n // inner
    w, z = lax.rem(me, inner), lax.div(me, inner)

    def mate(d):
        return lax.rem(w + d, inner)

    def far(e):
        return lax.rem(z + e, outer)

    def reach(to_z, to_w):
        return dict(device_id=(to_z * inner + to_w, band), device_id_type=MESH)

    partner = dict(device_id=(me, 1 - band), device_id_type=MESH)

    g, cols = trial_v.shape
    p_size = beta_v.shape[1]
    nbands = psi_v.shape[1]
    natom = cnt_ref.shape[1]
    mp = q_ref.shape[0] // maxp
    r1 = cols // n
    r2 = out_ref.shape[0]
    beta_chunks = beta_sem.shape[0]
    bw = p_size // beta_chunks
    psi_chunks = psi_sem.shape[0]
    pw = nbands // psi_chunks
    sw = 512

    def aligned(i, size):
        return pl.ds(i * size if isinstance(i, int) else pl.multiple_of(i * size, size), size)

    def beta_copy(c):
        at = (slice(None), pl.ds(c * bw, bw))
        return pltpu.make_async_copy(beta_h.at[at], beta_v.at[at], beta_sem.at[c])

    def psi_copy(c):
        at = (slice(None), pl.ds(c * pw, pw))
        return pltpu.make_async_copy(psi_h.at[at], psi_v.at[at], psi_sem.at[c])

    trial_copy = pltpu.make_async_copy(trial_h, trial_v, trial_sem)
    trial_copy.start()
    for c in range(beta_chunks):
        beta_copy(c).start()
    for c in range(psi_chunks):
        psi_copy(c).start()

    barrier = pltpu.get_barrier_semaphore()

    for d in range(1, inner):
        pl.semaphore_signal(barrier, inc=1, **reach(z, mate(d)))
    for e in range(1, outer):
        pl.semaphore_signal(barrier, inc=1, **reach(far(e), w))
    pl.semaphore_signal(barrier, inc=1, **partner)

    class Pair:
        def __init__(self, src, src_s, dst, dst_s, send, recv, to):
            self.both = [
                pltpu.make_async_remote_copy(
                    src_ref=a, dst_ref=b, send_sem=send.at[i], recv_sem=recv.at[i], **to
                )
                for i, (a, b) in enumerate(((src, dst), (src_s, dst_s)))
            ]

        def start(self):
            for copy in self.both:
                copy.start()

        def wait(self):
            for copy in self.both:
                copy.wait()

    def inner1(c, d):
        at = pl.ds(c * bw, bw)
        return Pair(
            code1.at[aligned(mate(d), outer * r1), at], scale1.at[c],
            in1.at[d, :, at], in1s.at[c, d],
            send1.at[c, d], recv1.at[c, d], reach(z, mate(d)),
        )

    def outer1(c, e):
        at = pl.ds(c * bw, bw)
        return Pair(
            code1b.at[far(e), :, at], scale1b.at[c],
            end1.at[e, :, at], end1s.at[c, e],
            send1b.at[c, e], recv1b.at[c, e], reach(far(e), w),
        )

    def middle1(c):
        at = pl.ds(c * bw, bw)
        total = proj[aligned(w, outer * r1), at]
        for d in range(1, inner):
            inner1(c, d).wait()
            total += decode(in1[d, :, at], in1s[c, d][:, :1])
        code, scale = encode(total)
        scale1b[c] = jnp.broadcast_to(scale, (1, 128))
        code1b[:, :, at] = code.reshape(outer, r1, bw)
        mid1[:, :, at] = total.reshape(outer, r1, bw)
        for e in range(1, outer):
            outer1(c, e).start()

    def diagonals(c, _):
        lanes = 256
        nd = qd.shape[0]
        ids = (c * lanes + lax.broadcasted_iota(jnp.int32, (natom, lanes), 1)).astype(F32)
        owns = (offs <= ids) & (ids < offs + own)
        pos = jnp.sum(jnp.where(owns, ids - offs, 0.0), axis=0, keepdims=True)
        count = jnp.sum(jnp.where(owns, jnp.broadcast_to(own, owns.shape), 0.0), axis=0, keepdims=True)
        pick = jnp.where(owns, 1.0, 0.0).astype(BF16)
        flat = jnp.dot(q_parts[0], pick, preferred_element_type=F32)
        flat += jnp.dot(q_parts[1], pick, preferred_element_type=F32)
        flat += jnp.dot(q_parts[2], pick, preferred_element_type=F32)
        q_row = jnp.zeros((mp, lanes), F32)
        for i in range(maxp):
            q_row += jnp.where(pos == float(i), flat[i * mp : (i + 1) * mp], 0.0)
        at = pos + lax.broadcasted_iota(jnp.int32, (nd, lanes), 0).astype(F32) - float(maxp - 1)
        entries = jnp.zeros((nd, lanes), F32)
        for j in range(maxp):
            entries += jnp.where(at == float(j), q_row[j : j + 1], 0.0)
        qd[:, aligned(c, lanes)] = jnp.where(at < count, entries, 0.0)
        return 0

    trial_copy.wait()

    def turn(k, _):
        trial_t[aligned(band, cols), aligned(k, sw)] = trial_v[aligned(k, sw), :].T
        return 0

    lax.fori_loop(0, g // sw, turn, 0)

    pl.semaphore_wait(barrier, inner + outer - 1)

    trial_x = pltpu.make_async_remote_copy(
        src_ref=trial_t.at[aligned(band, cols), :],
        dst_ref=trial_t.at[aligned(band, cols), :],
        send_sem=xs,
        recv_sem=xr,
        **partner,
    )
    trial_x.start()

    for c in range(beta_chunks):
        beta_copy(c).wait()
        at = pl.ds(c * bw, bw)
        part = jnp.dot(
            trial_t[aligned(band, cols), :], beta_v[:, at], preferred_element_type=F32
        )
        proj[:, at] = part
        code, scale = encode(part)
        code1[:, at] = code
        scale1[c] = jnp.broadcast_to(scale, (1, 128))
        for d in range(1, inner):
            inner1(c, d).start()

    def flip(c):
        def piece(k, _):
            beta_t[pl.ds(c * bw, bw), aligned(k, sw)] = beta_v[aligned(k, sw), pl.ds(c * bw, bw)].T
            return 0

        lax.fori_loop(0, g // sw, piece, 0)

    flip(0)

    cnt = cnt_ref[...].astype(F32)
    row = lax.broadcasted_iota(jnp.int32, (natom, natom), 0)
    col = lax.broadcasted_iota(jnp.int32, (natom, natom), 1)
    offs = jnp.sum(jnp.where(col < row, cnt, 0.0), axis=1, keepdims=True)
    own = jnp.sum(jnp.where(col == row, cnt, 0.0), axis=1, keepdims=True)
    q = q_ref[...]
    q_hi = q.astype(BF16)
    rest = q - q_hi.astype(F32)
    q_mid = rest.astype(BF16)
    q_parts[0] = q_hi
    q_parts[1] = q_mid
    q_parts[2] = (rest - q_mid.astype(F32)).astype(BF16)
    lax.fori_loop(0, p_size // 256, diagonals, 0)

    middle1(0)

    trial_x.wait()
    for c in range(psi_chunks):
        psi_copy(c).wait()

    def plain(c, _):
        got = jnp.dot(trial_t[...], psi_v[:, aligned(c, pw)], preferred_element_type=F32)
        fin[:, :, :, aligned(c, pw)] = got.reshape(outer, inner, r2, pw)
        return 0

    def bands(c):
        def piece(k, _):
            at = (pl.ds(c * bw, bw), aligned(k, pw))
            got = jnp.dot(
                beta_t[pl.ds(c * bw, bw), :], psi_v[:, aligned(k, pw)], preferred_element_type=F32
            )
            hi, lo = split2(got)
            g_hi[at] = hi
            g_lo[at] = lo
            return 0

        lax.fori_loop(0, psi_chunks, piece, 0)

    lax.fori_loop(0, psi_chunks, plain, 0)
    for c in range(1, beta_chunks):
        middle1(c)

    bands(0)

    for c in range(beta_chunks):
        for e in range(1, outer):
            outer1(c, e).wait()
    pieces = []
    for c in range(beta_chunks):
        at = pl.ds(c * bw, bw)
        piece = mid1[z, :, at]
        for e in range(1, outer):
            piece += decode(end1[e, :, at], end1s[c, e][:, :1])
        pieces.append(piece)
    x = jnp.concatenate(pieces, axis=1)
    acc = jnp.zeros_like(x)
    for d in range(2 * maxp - 1):
        shift = (maxp - 1 - d) % p_size
        moved = x if shift == 0 else pltpu.roll(x, shift, axis=1)
        acc += qd[d : d + 1, :] * moved
    mine = w * outer + z
    code, scale = encode(acc)
    wall[band, mine] = code
    walls[band, mine] = jnp.broadcast_to(scale, (1, 128))

    def outer2(e):
        return Pair(
            wall.at[band, mine], walls.at[band, mine], wall.at[band, mine], walls.at[band, mine],
            send2.at[e], recv2.at[e], reach(far(e), w),
        )

    def inner2(e, d):
        block = w * outer + lax.rem(z + outer - e, outer)
        return Pair(
            wall.at[band, block], walls.at[band, block], wall.at[band, block], walls.at[band, block],
            send2b.at[e, d], recv2b.at[e, d], reach(z, mate(d)),
        )

    def across(d):
        rows = aligned(lax.rem(w + inner - d, inner), outer)
        return Pair(
            wall.at[band, rows], walls.at[band, rows], wall.at[band, rows], walls.at[band, rows],
            send2c.at[d], recv2c.at[d], partner,
        )

    for e in range(1, outer):
        outer2(e).start()
    for d in range(1, inner):
        inner2(0, d).start()

    flip(1)
    bands(1)
    for e in range(1, outer):
        outer2(e).wait()
        for d in range(1, inner):
            inner2(e, d).start()
    across(0).start()
    flip(2)
    bands(2)

    for d in range(1, inner):
        for e in range(outer):
            inner2(e, d).wait()
        across(d).start()
    for d in range(inner):
        across(d).wait()

    def spread(i, _):
        for b in range(2):
            both = [decode(wall[b, 2 * i + j], walls[b, 2 * i + j][:, :1]) for j in range(2)]
            hi, lo = split2(jnp.concatenate(both, axis=0))
            at = pl.ds(pl.multiple_of(b * cols + i * 2 * r1, 2 * r1), 2 * r1)
            w_hi[at, :] = hi
            w_lo[at, :] = lo
        return 0

    lax.fori_loop(0, n // 2, spread, 0)

    def inner3(c, d):
        return Pair(
            code3.at[:, mate(d), :, aligned(c, pw)], scale3.at[c],
            in3.at[d, :, :, aligned(c, pw)], in3s.at[c, d],
            send3.at[c, d], recv3.at[c, d], reach(z, mate(d)),
        )

    def outer3(c, e):
        return Pair(
            code3b.at[far(e), :, aligned(c, pw)], scale3b.at[c],
            end3.at[e, :, aligned(c, pw)], end3s.at[c, e],
            send3b.at[c, e], recv3b.at[c, e], reach(far(e), w),
        )

    def middle3(c):
        at = aligned(c, pw)
        for d in range(1, inner):
            inner3(c, d).wait()
        total = fin[:, w, :, at].reshape(outer * r2, pw)
        for d in range(1, inner):
            total += decode(in3[d, :, :, at].reshape(outer * r2, pw), in3s[c, d][:, :1])
        code, scale = encode(total)
        scale3b[c] = jnp.broadcast_to(scale, (1, 128))
        code3b[:, :, at] = code.reshape(outer, r2, pw)
        mid3[:, :, at] = total.reshape(outer, r2, pw)
        for e in range(1, outer):
            outer3(c, e).start()

    def share(c):
        at = aligned(c, pw)
        f = jnp.dot(w_hi[...], g_hi[:, at], preferred_element_type=F32)
        f += jnp.dot(w_hi[...], g_lo[:, at], preferred_element_type=F32)
        f += jnp.dot(w_lo[...], g_hi[:, at], preferred_element_type=F32)
        f += fin[:, :, :, at].reshape(2 * cols, pw)
        code, scale = encode(f)
        scale3[c] = jnp.broadcast_to(scale, (1, 128))
        code3[:, :, :, at] = code.reshape(outer, inner, r2, pw)
        fin[:, :, :, at] = f.reshape(outer, inner, r2, pw)
        for d in range(1, inner):
            inner3(c, d).start()

    for c in range(psi_chunks):
        share(c)
        if c:
            middle3(c - 1)
    middle3(psi_chunks - 1)

    for c in range(psi_chunks):
        at = aligned(c, pw)
        total = mid3[z, :, at]
        for e in range(1, outer):
            outer3(c, e).wait()
            total += decode(end3[e, :, at], end3s[c, e][:, :1])
        out_ref[:, at] = total


def fused(n, inner, blk, psi, trial, beta, q_blocks, atom_counts):
    g, cols = trial.shape
    nbands = psi.shape[1]
    p_size = beta.shape[1]
    natom, maxp = q_blocks.shape[:2]
    mp = -(-maxp // 8) * 8
    nd = -(-(2 * maxp - 1) // 8) * 8
    r1, r2 = cols // n, blk // n
    outer = n // inner
    bc, pc = 3, 4
    q_flat = jnp.pad(q_blocks, ((0, 0), (0, 0), (0, mp - maxp)))
    q_flat = q_flat.transpose(1, 2, 0).reshape(maxp * mp, natom)
    dma = pltpu.SemaphoreType.DMA
    vm = pltpu.VMEM
    out = pl.pallas_call(
        functools.partial(kernel, n, inner, maxp),
        out_shape=jax.ShapeDtypeStruct((r2, nbands), F32),
        in_specs=[pl.BlockSpec(memory_space=pl.ANY)] * 3
        + [pl.BlockSpec(memory_space=pltpu.VMEM)] * 2,
        out_specs=pl.BlockSpec(memory_space=pltpu.VMEM),
        scratch_shapes=[
            vm((g, nbands), BF16),
            vm((g, p_size), BF16),
            vm((g, cols), BF16),
            vm((p_size, g), BF16),
            vm((blk, g), BF16),
            vm((3, maxp * mp, natom), BF16),
            vm((nd, p_size), F32),
            vm((p_size, nbands), BF16),
            vm((p_size, nbands), BF16),
            vm((blk, p_size), BF16),
            vm((blk, p_size), BF16),
            vm((cols, p_size), F32),
            vm((cols, p_size), I16),
            vm((bc, 1, 128), F32),
            vm((inner, outer * r1, p_size), I16),
            vm((bc, inner, 1, 128), F32),
            vm((outer, r1, p_size), F32),
            vm((outer, r1, p_size), I16),
            vm((bc, 1, 128), F32),
            vm((outer, r1, p_size), I16),
            vm((bc, outer, 1, 128), F32),
            vm((2, n, r1, p_size), I16),
            vm((2, n, 1, 128), F32),
            vm((outer, inner, r2, nbands), F32),
            vm((outer, inner, r2, nbands), I16),
            vm((pc, 1, 128), F32),
            vm((inner, outer, r2, nbands), I16),
            vm((pc, inner, 1, 128), F32),
            vm((outer, r2, nbands), F32),
            vm((outer, r2, nbands), I16),
            vm((pc, 1, 128), F32),
            vm((outer, r2, nbands), I16),
            vm((pc, outer, 1, 128), F32),
            dma,
            dma((bc,)),
            dma((pc,)),
            dma,
            dma,
            dma((bc, inner, 2)),
            dma((bc, inner, 2)),
            dma((bc, outer, 2)),
            dma((bc, outer, 2)),
            dma((outer, 2)),
            dma((outer, 2)),
            dma((outer, inner, 2)),
            dma((outer, inner, 2)),
            dma((inner, 2)),
            dma((inner, 2)),
            dma((pc, inner, 2)),
            dma((pc, inner, 2)),
            dma((pc, outer, 2)),
            dma((pc, outer, 2)),
        ],
        compiler_params=pltpu.CompilerParams(
            collective_id=0, has_side_effects=True, vmem_limit_bytes=62 * 1024 * 1024
        ),
    )(psi, trial, beta, q_flat, atom_counts.reshape(1, natom))
    return out.T


def q_dense(atom_counts, q_blocks, p_size):
    offsets = jnp.cumsum(atom_counts, dtype=jnp.int32) - atom_counts
    natom, maxp = q_blocks.shape[:2]
    ids = jnp.arange(p_size, dtype=jnp.int32)
    owns = (offsets[None, :] <= ids[:, None]) & (ids[:, None] < (offsets + atom_counts)[None, :])
    pos = jnp.sum(jnp.where(owns, ids[:, None] - offsets[None, :], 0), axis=1)
    atom = jnp.sum(jnp.where(owns, jnp.arange(natom, dtype=jnp.int32)[None, :], 0), axis=1)
    flat = jnp.dot(owns.astype(F32), q_blocks.reshape(natom, maxp * maxp), precision=precise)
    place = pos[:, None] == jnp.arange(maxp, dtype=jnp.int32)[None, :]
    rows = jnp.sum(jnp.where(place[:, :, None], flat.reshape(p_size, maxp, maxp), 0.0), axis=1)
    entries = jnp.dot(rows, place.astype(F32).T, precision=precise)
    return jnp.where(atom[:, None] == atom[None, :], entries, 0.0)


def general(psi, trial, beta, q_blocks, atom_counts):
    own = lax.psum(contract(beta, trial), "ga")
    weighted = jnp.dot(q_dense(atom_counts, q_blocks, beta.shape[1]), own, precision=precise)
    w_hi, w_lo = split2(weighted)
    both = jnp.dot(beta, jnp.concatenate([w_hi, w_lo], axis=1), preferred_element_type=F32)
    cols = trial.shape[1]
    s = both[:, :cols] + both[:, cols:] + trial.astype(F32)
    s_hi, s_lo = split2(lax.all_gather(s, "band", axis=1, tiled=True))
    part = contract(psi, s_hi) + contract(psi, s_lo)
    return lax.psum_scatter(part, "ga", scatter_dimension=1, tiled=True)


def solution(mesh):
    n, bands = mesh.shape["ga"], mesh.shape["band"]
    inner = 4

    def shards(psi, trial, beta, q_blocks, atom_counts):
        g, cols = trial.shape
        blk = cols * bands
        fits = (
            bands == 2
            and n % (2 * inner) == 0
            and cols % 128 == 0
            and cols % (8 * n) == 0
            and blk % (8 * n) == 0
            and g % 4096 == 0
            and beta.shape[1] % 768 == 0
            and psi.shape[1] % 512 == 0
            and q_blocks.shape[0] % 128 == 0
        )
        if fits:
            return fused(n, inner, blk, psi, trial, beta, q_blocks, atom_counts)
        return general(psi, trial, beta, q_blocks, atom_counts)

    in_specs = (P("ga", "band"), P("ga", "band"), P("ga", None), P(), P())
    out_specs = P("band", "ga")
    return jax.shard_map(shards, mesh=mesh, in_specs=in_specs, out_specs=out_specs, check_vma=False)
```

time: 68.5 us -> 67.3 us (0.982)
  Pallas kernels: 65.2 us -> 63.9 us
    pallas_call x1, Pallas kernels: 65.2 us -> 63.9 us  [fused(): pl.pallas_call(functools.partial(kernel, n, inner, maxp), out_shape=jax.S...]
where the time goes in v1:
time: 67.3 us; the launch traced here: 67.1 us
  Pallas kernels  63.9 us (95%)
  local copies, waits for them, and re-layouts  3.1 us (5%)
    pallas_call x1, Pallas kernels, fused(): pl.pallas_call(functools.partial(kernel, n, inner, maxp), out_shape=jax.S...  63.9 us
    pad x1, local copies, waits for them, and re-layouts, fused(): q_flat = jnp.pad(q_blocks, ((0, 0), (0, 0), (0, mp - maxp)))  1.62 us
    unnamed x1, local copies, waits for them, and re-layouts  1.47 us

profile of v1, /device:TPU:0, one launch (start us, length us, event | category | flops | bytes accessed | tf_op | source)
XLA Modules:
  0.0 67.1 jit_solution(11148833027555940602)
XLA Ops:
  0.0 1.6 %pad.4 = f32[128,18,24]{0,2,1:T(8,128)} pad(f32[128,18,18]{0,2,1:T(8,128)} %param.8, f32[]{:T(128)} %constant.2.clone.1), padding=0_0x0_0x0_6 | pad | bytes 387076 | tf_op jit(solution)/shard_map/jit(_pad)/pad | solution.py:392
  1.6 63.9 %shard_map.55 = f32[16,1024]{1,0:T(8,128)} custom-call(bf16[4096,1024]{1,0:T(8,128)(2,1)} %psi_h.1, bf16[4096,128]{1,0:T(8,128)(2,1)} %trial_h.1, bf16[4096,1536]{1,0:T(8,128)(2,1)} %beta_h.1, f32[432,128]{1,0:T(8,128)} %bitcast.5, s32[1,128]{1,0:T(1,128)} %bitcast.7), custom_call_target="tpu_custom_call" | custom-call | tf_op jit(solution)/shard_map/pallas_call | solution.py:396
  65.6 1.5 %copy.7 = f32[1024,16]{0,1:T(8,128)} copy(f32[1024,16]{0,1:T(8,128)} %bitcast.6) | data formatting | bytes 131072

commit v2 on v1

v2 whole, which is shorter than its diff:
```python
import functools

import jax
import jax.numpy as jnp
from jax import lax
from jax.experimental import pallas as pl
from jax.experimental.pallas import tpu as pltpu
from jax.sharding import PartitionSpec as P

MESH = pl.DeviceIdType.MESH
precise = lax.Precision.HIGHEST
F32, BF16, I16 = jnp.float32, jnp.bfloat16, jnp.int16
LEVELS, TINY = 32767.0, 1e-30


def contract(left, right, precision=None):
    return lax.dot_general(
        left, right, (((0,), (0,)), ((), ())), precision=precision, preferred_element_type=F32
    )


def split2(x):
    hi = x.astype(BF16)
    return hi, (x - hi.astype(F32)).astype(BF16)


def encode(x):
    top = jnp.maximum(jnp.max(jnp.abs(x), keepdims=True), TINY)
    return jnp.round(x * (LEVELS / top)).astype(jnp.int32).astype(I16), top * (1.0 / LEVELS)


def decode(code, scale):
    return code.astype(jnp.int32).astype(F32) * scale


def kernel(
    n, inner, maxp, psi_h, trial_h, beta_h, q_h, cnt_h, out_ref,
    psi_v, beta_v, trial_v, q_v, cnt_v, beta_t, trial_t, q_parts, qd, g_hi, g_lo, w_hi, w_lo,
    proj, code1, scale1, in1, in1s, mid1, code1b, scale1b, end1, end1s,
    wall, walls, fin, code3, scale3, in3, in3s, mid3, code3b, scale3b, end3, end3s,
    q_sem, trial_sem, beta_sem, psi_sem, xs, xr, sent, recv1, recv1b, recv2, recv2b, recv2c,
    recv3, recv3b,
):
    me = lax.axis_index("ga")
    band = lax.axis_index("band")
    outer = n // inner
    w, z = lax.rem(me, inner), lax.div(me, inner)

    def mate(d):
        x, y = lax.rem(w, 2), lax.div(w, 2)
        return lax.rem(x + d % 2, 2) + 2 * lax.rem(y + d // 2, 2)

    def far(e):
        return lax.rem(z + e, outer)

    def reach(to_z, to_w):
        return dict(device_id=(to_z * inner + to_w, band), device_id_type=MESH)

    partner = dict(device_id=(me, 1 - band), device_id_type=MESH)
    mates = tuple(range(inner - 1, 0, -1))
    fars = tuple(range(1, outer))

    g, cols = trial_v.shape
    p_size = beta_v.shape[1]
    nbands = psi_v.shape[1]
    natom = cnt_v.shape[1]
    mp = q_parts.shape[1] // maxp
    r1 = cols // n
    r2 = out_ref.shape[0]
    beta_chunks = beta_sem.shape[0]
    bw = p_size // beta_chunks
    psi_chunks = psi_sem.shape[0]
    pw = nbands // psi_chunks
    sw = 512

    def aligned(i, size):
        return pl.ds(i * size if isinstance(i, int) else pl.multiple_of(i * size, size), size)

    def beta_copy(c):
        at = (slice(None), pl.ds(c * bw, bw))
        return pltpu.make_async_copy(beta_h.at[at], beta_v.at[at], beta_sem.at[c])

    def psi_copy(c):
        at = (slice(None), pl.ds(c * pw, pw))
        return pltpu.make_async_copy(psi_h.at[at], psi_v.at[at], psi_sem.at[c])

    q_copy = pltpu.make_async_copy(q_h, q_v, q_sem.at[0])
    cnt_copy = pltpu.make_async_copy(cnt_h, cnt_v, q_sem.at[1])
    trial_copy = pltpu.make_async_copy(trial_h, trial_v, trial_sem)
    q_copy.start()
    cnt_copy.start()
    trial_copy.start()
    beta_copy(0).start()

    barrier = pltpu.get_barrier_semaphore()

    for d in mates:
        pl.semaphore_signal(barrier, inc=1, **reach(z, mate(d)))
    for e in fars:
        pl.semaphore_signal(barrier, inc=1, **reach(far(e), w))
    pl.semaphore_signal(barrier, inc=1, **partner)

    def send(stage, src, src_s, dst, dst_s, recv, to):
        for i, (a, b) in enumerate(((src, dst), (src_s, dst_s))):
            pltpu.make_async_remote_copy(
                src_ref=a, dst_ref=b, send_sem=sent.at[stage, i], recv_sem=recv.at[i], **to
            ).start()

    def landed(ref, ref_s, recv):
        for i, a in enumerate((ref, ref_s)):
            pltpu.make_async_remote_copy(
                src_ref=a, dst_ref=a, send_sem=sent.at[0, i], recv_sem=recv.at[i], **partner
            ).wait_recv()

    def left(stage, ref, ref_s):
        for i, a in enumerate((ref, ref_s)):
            pltpu.make_async_remote_copy(
                src_ref=a, dst_ref=a, send_sem=sent.at[stage, i], recv_sem=recv1.at[0, i], **partner
            ).wait_send()

    def middle1(c):
        at = pl.ds(c * bw, bw)
        landed(in1.at[pl.ds(1, inner - 1), :, at], in1s.at[c, pl.ds(1, inner - 1)], recv1.at[c])
        total = proj[aligned(w, outer * r1), at]
        for d in mates:
            total += decode(in1[d, :, at], in1s[c, d][:, :1])
        code, scale = encode(total)
        scale1b[c] = jnp.broadcast_to(scale, (1, 128))
        code1b[:, :, at] = code.reshape(outer, r1, bw)
        mid1[:, :, at] = total.reshape(outer, r1, bw)
        for e in fars:
            send(
                1, code1b.at[far(e), :, at], scale1b.at[c],
                end1.at[e, :, at], end1s.at[c, e], recv1b.at[c], reach(far(e), w),
            )

    with jax.named_scope("q_wait"):
        q_copy.wait()
        cnt_copy.wait()
    with jax.named_scope("diag"):
        cnt = cnt_v[...].astype(F32)
        row = lax.broadcasted_iota(jnp.int32, (natom, natom), 0)
        col = lax.broadcasted_iota(jnp.int32, (natom, natom), 1)
        offs = jnp.sum(jnp.where(col < row, cnt, 0.0), axis=1, keepdims=True)
        own = jnp.sum(jnp.where(col == row, cnt, 0.0), axis=1, keepdims=True)
        q_parts[...] = jnp.zeros_like(q_parts)
        for i in range(maxp):
            q = q_v[i]
            q_hi = q.astype(BF16)
            rest = q - q_hi.astype(F32)
            q_mid = rest.astype(BF16)
            at = slice(i * mp, i * mp + maxp)
            q_parts[0, at] = q_hi
            q_parts[1, at] = q_mid
            q_parts[2, at] = (rest - q_mid.astype(F32)).astype(BF16)

        def diagonals(c, _):
            lanes = 256
            nd = qd.shape[0]
            ids = (c * lanes + lax.broadcasted_iota(jnp.int32, (natom, lanes), 1)).astype(F32)
            owns = (offs <= ids) & (ids < offs + own)
            pos = jnp.sum(jnp.where(owns, ids - offs, 0.0), axis=0, keepdims=True)
            count = jnp.sum(
                jnp.where(owns, jnp.broadcast_to(own, owns.shape), 0.0), axis=0, keepdims=True
            )
            pick = jnp.where(owns, 1.0, 0.0).astype(BF16)
            flat = jnp.dot(q_parts[0], pick, preferred_element_type=F32)
            flat += jnp.dot(q_parts[1], pick, preferred_element_type=F32)
            flat += jnp.dot(q_parts[2], pick, preferred_element_type=F32)
            q_row = jnp.zeros((mp, lanes), F32)
            for i in range(maxp):
                q_row += jnp.where(pos == float(i), flat[i * mp : (i + 1) * mp], 0.0)
            at = pos + lax.broadcasted_iota(jnp.int32, (nd, lanes), 0).astype(F32) - float(maxp - 1)
            entries = jnp.zeros((nd, lanes), F32)
            for j in range(maxp):
                entries += jnp.where(at == float(j), q_row[j : j + 1], 0.0)
            qd[:, aligned(c, lanes)] = jnp.where(at < count, entries, 0.0)
            return 0

        lax.fori_loop(0, p_size // 256, diagonals, 0)

    with jax.named_scope("trial_wait"):
        trial_copy.wait()
    beta_copy(1).start()

    def turn(k, _):
        trial_t[aligned(band, cols), aligned(k, sw)] = trial_v[aligned(k, sw), :].T
        return 0

    with jax.named_scope("turn"):
        lax.fori_loop(0, g // sw, turn, 0)

    with jax.named_scope("barrier"):
        pl.semaphore_wait(barrier, inner + outer - 1)

    trial_x = pltpu.make_async_remote_copy(
        src_ref=trial_t.at[aligned(band, cols), :],
        dst_ref=trial_t.at[aligned(band, cols), :],
        send_sem=xs,
        recv_sem=xr,
        **partner,
    )
    trial_x.start()

    for c in range(beta_chunks):
        with jax.named_scope(f"load_{c}"):
            beta_copy(c).wait()
        if c + 2 < beta_chunks:
            beta_copy(c + 2).start()
        elif c + 2 == beta_chunks:
            for k in range(psi_chunks):
                psi_copy(k).start()
        at = pl.ds(c * bw, bw)
        with jax.named_scope(f"p1_{c}"):
            part = jnp.dot(
                trial_t[aligned(band, cols), :], beta_v[:, at], preferred_element_type=F32
            )
            proj[:, at] = part
            code, scale = encode(part)
            code1[:, at] = code
            scale1[c] = jnp.broadcast_to(scale, (1, 128))
            for d in mates:
                send(
                    0, code1.at[aligned(mate(d), outer * r1), at], scale1.at[c],
                    in1.at[d, :, at], in1s.at[c, d], recv1.at[c], reach(z, mate(d)),
                )

    def flip(c):
        def piece(k, _):
            beta_t[pl.ds(c * bw, bw), aligned(k, sw)] = beta_v[aligned(k, sw), pl.ds(c * bw, bw)].T
            return 0

        with jax.named_scope(f"flip_{c}"):
            lax.fori_loop(0, g // sw, piece, 0)

    def plain(c, _):
        got = jnp.dot(trial_t[...], psi_v[:, aligned(c, pw)], preferred_element_type=F32)
        fin[:, :, :, aligned(c, pw)] = got.reshape(outer, inner, r2, pw)
        return 0

    def bands(c):
        step = bw // psi_chunks

        def piece(k, _):
            at = (pl.ds(c * bw, bw), aligned(k, pw))
            if c + 1 < beta_chunks:
                part = pl.ds(pl.multiple_of((c + 1) * bw + k * step, step), step)
                beta_t[part, :] = beta_v[:, part].T
            got = jnp.dot(
                beta_t[pl.ds(c * bw, bw), :], psi_v[:, aligned(k, pw)], preferred_element_type=F32
            )
            hi, lo = split2(got)
            g_hi[at] = hi
            g_lo[at] = lo
            return 0

        with jax.named_scope(f"bands_{c}"):
            lax.fori_loop(0, psi_chunks, piece, 0)

    flip(0)
    with jax.named_scope("psi_wait"):
        trial_x.wait()
        for c in range(psi_chunks):
            psi_copy(c).wait()
    with jax.named_scope("plain"):
        lax.fori_loop(0, psi_chunks, plain, 0)
    for c in range(beta_chunks):
        with jax.named_scope(f"mid1_{c}"):
            middle1(c)
    bands(0)

    with jax.named_scope("wait_z1"):
        for c in range(beta_chunks):
            at = pl.ds(c * bw, bw)
            landed(
                end1.at[pl.ds(1, outer - 1), :, at], end1s.at[c, pl.ds(1, outer - 1)], recv1b.at[c]
            )

    mine = w * outer + z
    with jax.named_scope("q_apply"):
        pieces = []
        for c in range(beta_chunks):
            at = pl.ds(c * bw, bw)
            piece = mid1[z, :, at]
            for e in fars:
                piece += decode(end1[e, :, at], end1s[c, e][:, :1])
            pieces.append(piece)
        x = jnp.concatenate(pieces, axis=1)
        acc = jnp.zeros_like(x)
        for d in range(2 * maxp - 1):
            shift = (maxp - 1 - d) % p_size
            moved = x if shift == 0 else pltpu.roll(x, shift, axis=1)
            acc += qd[d : d + 1, :] * moved
        code, scale = encode(acc)
        wall[band, mine] = code
        walls[band, mine] = jnp.broadcast_to(scale, (1, 128))

    def share_w(stage, rows, recv, to):
        a, b = wall.at[band, rows], walls.at[band, rows]
        send(stage, a, b, a, b, recv, to)

    for e in fars:
        share_w(2, mine, recv2.at[e - 1], reach(far(e), w))
    for d in mates:
        share_w(3, mine, recv2b.at[d - 1], reach(z, mate(d)))

    bands(1)
    with jax.named_scope("ag_z"):
        for e in fars:
            block = w * outer + lax.rem(z + outer - e, outer)
            landed(wall.at[band, block], walls.at[band, block], recv2.at[e - 1])
            for d in mates:
                share_w(3, block, recv2b.at[d - 1], reach(z, mate(d)))
        share_w(4, aligned(w, outer), recv2c.at[0], partner)
    bands(2)

    with jax.named_scope("ag_xy"):
        for d in (1, 2, 3):
            rows = aligned(mate(d), outer)
            landed(wall.at[band, rows], walls.at[band, rows], recv2b.at[d - 1])
            share_w(4, rows, recv2c.at[d], partner)
        for d in range(inner):
            rows = aligned(mate(d), outer)
            landed(wall.at[1 - band, rows], walls.at[1 - band, rows], recv2c.at[d])

    def spread(i, _):
        for b in range(2):
            both = [decode(wall[b, 2 * i + j], walls[b, 2 * i + j][:, :1]) for j in range(2)]
            hi, lo = split2(jnp.concatenate(both, axis=0))
            at = pl.ds(pl.multiple_of(b * cols + i * 2 * r1, 2 * r1), 2 * r1)
            w_hi[at, :] = hi
            w_lo[at, :] = lo
        return 0

    with jax.named_scope("spread"):
        lax.fori_loop(0, n // 2, spread, 0)

    def middle3(c):
        at = aligned(c, pw)
        others = pl.ds(1, inner - 1)
        landed(in3.at[others, :, :, at], in3s.at[c, others], recv3.at[c])
        total = fin[:, w, :, at].reshape(outer * r2, pw)
        for d in mates:
            total += decode(in3[d, :, :, at].reshape(outer * r2, pw), in3s[c, d][:, :1])
        code, scale = encode(total)
        scale3b[c] = jnp.broadcast_to(scale, (1, 128))
        code3b[:, :, at] = code.reshape(outer, r2, pw)
        mid3[:, :, at] = total.reshape(outer, r2, pw)
        for e in fars:
            send(
                6, code3b.at[far(e), :, at], scale3b.at[c],
                end3.at[e, :, at], end3s.at[c, e], recv3b.at[c], reach(far(e), w),
            )

    def share(c):
        at = aligned(c, pw)
        f = jnp.dot(w_hi[...], g_hi[:, at], preferred_element_type=F32)
        f += jnp.dot(w_hi[...], g_lo[:, at], preferred_element_type=F32)
        f += jnp.dot(w_lo[...], g_hi[:, at], preferred_element_type=F32)
        f += fin[:, :, :, at].reshape(2 * cols, pw)
        code, scale = encode(f)
        scale3[c] = jnp.broadcast_to(scale, (1, 128))
        code3[:, :, :, at] = code.reshape(outer, inner, r2, pw)
        fin[:, :, :, at] = f.reshape(outer, inner, r2, pw)
        for d in mates:
            send(
                5, code3.at[:, mate(d), :, at], scale3.at[c],
                in3.at[d, :, :, at], in3s.at[c, d], recv3.at[c], reach(z, mate(d)),
            )

    for c in range(psi_chunks):
        with jax.named_scope(f"share_{c}"):
            share(c)
    for c in range(psi_chunks):
        with jax.named_scope(f"mid3_{c}"):
            middle3(c)

    with jax.named_scope("tail"):
        others = pl.ds(1, outer - 1)
        for c in range(psi_chunks):
            at = aligned(c, pw)
            landed(end3.at[others, :, at], end3s.at[c, others], recv3b.at[c])
            total = mid3[z, :, at]
            for e in fars:
                total += decode(end3[e, :, at], end3s[c, e][:, :1])
            out_ref[:, at] = total

    with jax.named_scope("drain"):
        k, m = pl.ds(0, inner - 1), pl.ds(0, outer - 1)
        left(0, code1.at[pl.ds(0, (inner - 1) * outer * r1), :], in1s.at[:, k])
        left(1, code1b.at[m], end1s.at[:, m])
        left(2, wall.at[0, m], walls.at[0, m])
        rows = pl.ds(0, (inner - 1) * outer)
        left(3, wall.at[0, rows], walls.at[0, rows])
        left(4, wall.at[0], walls.at[0])
        left(5, code3.at[:, k], in3s.at[:, k])
        left(6, code3b.at[m], end3s.at[:, m])


def fused(n, inner, blk, psi, trial, beta, q_blocks, atom_counts):
    g, cols = trial.shape
    nbands = psi.shape[1]
    p_size = beta.shape[1]
    natom, maxp = q_blocks.shape[:2]
    mp = -(-maxp // 8) * 8
    nd = -(-(2 * maxp - 1) // 8) * 8
    r1, r2 = cols // n, blk // n
    outer = n // inner
    bc, pc = 3, 4
    dma = pltpu.SemaphoreType.DMA
    vm = pltpu.VMEM
    out = pl.pallas_call(
        functools.partial(kernel, n, inner, maxp),
        out_shape=jax.ShapeDtypeStruct((r2, nbands), F32),
        in_specs=[pl.BlockSpec(memory_space=pl.ANY)] * 5,
        out_specs=pl.BlockSpec(memory_space=pltpu.VMEM),
        scratch_shapes=[
            vm((g, nbands), BF16),
            vm((g, p_size), BF16),
            vm((g, cols), BF16),
            vm((maxp, maxp, natom), F32),
            vm((1, natom), jnp.int32),
            vm((p_size, g), BF16),
            vm((blk, g), BF16),
            vm((3, maxp * mp, natom), BF16),
            vm((nd, p_size), F32),
            vm((p_size, nbands), BF16),
            vm((p_size, nbands), BF16),
            vm((blk, p_size), BF16),
            vm((blk, p_size), BF16),
            vm((cols, p_size), F32),
            vm((cols, p_size), I16),
            vm((bc, 1, 128), F32),
            vm((inner, outer * r1, p_size), I16),
            vm((bc, inner, 1, 128), F32),
            vm((outer, r1, p_size), F32),
            vm((outer, r1, p_size), I16),
            vm((bc, 1, 128), F32),
            vm((outer, r1, p_size), I16),
            vm((bc, outer, 1, 128), F32),
            vm((2, n, r1, p_size), I16),
            vm((2, n, 1, 128), F32),
            vm((outer, inner, r2, nbands), F32),
            vm((outer, inner, r2, nbands), I16),
            vm((pc, 1, 128), F32),
            vm((inner, outer, r2, nbands), I16),
            vm((pc, inner, 1, 128), F32),
            vm((outer, r2, nbands), F32),
            vm((outer, r2, nbands), I16),
            vm((pc, 1, 128), F32),
            vm((outer, r2, nbands), I16),
            vm((pc, outer, 1, 128), F32),
            dma((2,)),
            dma,
            dma((bc,)),
            dma((pc,)),
            dma,
            dma,
            dma((7, 2)),
            dma((bc, 2)),
            dma((bc, 2)),
            dma((outer - 1, 2)),
            dma((inner - 1, 2)),
            dma((inner, 2)),
            dma((pc, 2)),
            dma((pc, 2)),
        ],
        compiler_params=pltpu.CompilerParams(
            collective_id=0, has_side_effects=True, vmem_limit_bytes=62 * 1024 * 1024
        ),
    )(psi, trial, beta, q_blocks.transpose(1, 2, 0), atom_counts.reshape(1, natom))
    return out.T


def q_dense(atom_counts, q_blocks, p_size):
    offsets = jnp.cumsum(atom_counts, dtype=jnp.int32) - atom_counts
    natom, maxp = q_blocks.shape[:2]
    ids = jnp.arange(p_size, dtype=jnp.int32)
    owns = (offsets[None, :] <= ids[:, None]) & (ids[:, None] < (offsets + atom_counts)[None, :])
    pos = jnp.sum(jnp.where(owns, ids[:, None] - offsets[None, :], 0), axis=1)
    atom = jnp.sum(jnp.where(owns, jnp.arange(natom, dtype=jnp.int32)[None, :], 0), axis=1)
    flat = jnp.dot(owns.astype(F32), q_blocks.reshape(natom, maxp * maxp), precision=precise)
    place = pos[:, None] == jnp.arange(maxp, dtype=jnp.int32)[None, :]
    rows = jnp.sum(jnp.where(place[:, :, None], flat.reshape(p_size, maxp, maxp), 0.0), axis=1)
    entries = jnp.dot(rows, place.astype(F32).T, precision=precise)
    return jnp.where(atom[:, None] == atom[None, :], entries, 0.0)


def general(psi, trial, beta, q_blocks, atom_counts):
    own = lax.psum(contract(beta, trial), "ga")
    weighted = jnp.dot(q_dense(atom_counts, q_blocks, beta.shape[1]), own, precision=precise)
    w_hi, w_lo = split2(weighted)
    both = jnp.dot(beta, jnp.concatenate([w_hi, w_lo], axis=1), preferred_element_type=F32)
    cols = trial.shape[1]
    s = both[:, :cols] + both[:, cols:] + trial.astype(F32)
    s_hi, s_lo = split2(lax.all_gather(s, "band", axis=1, tiled=True))
    part = contract(psi, s_hi) + contract(psi, s_lo)
    return lax.psum_scatter(part, "ga", scatter_dimension=1, tiled=True)


def solution(mesh):
    n, bands = mesh.shape["ga"], mesh.shape["band"]
    inner = 4

    def shards(psi, trial, beta, q_blocks, atom_counts):
        g, cols = trial.shape
        blk = cols * bands
        fits = (
            bands == 2
            and n % (2 * inner) == 0
            and cols % 128 == 0
            and cols % (8 * n) == 0
            and blk % (8 * n) == 0
            and g % 4096 == 0
            and beta.shape[1] % 768 == 0
            and psi.shape[1] % 512 == 0
            and q_blocks.shape[0] % 128 == 0
        )
        if fits:
            return fused(n, inner, blk, psi, trial, beta, q_blocks, atom_counts)
        return general(psi, trial, beta, q_blocks, atom_counts)

    in_specs = (P("ga", "band"), P("ga", "band"), P("ga", None), P(), P())
    out_specs = P("band", "ga")
    return jax.shard_map(shards, mesh=mesh, in_specs=in_specs, out_specs=out_specs, check_vma=False)
```

time: 67.3 us -> 54.8 us (0.81)
  Pallas kernels: 63.9 us -> 53.2 us
  local copies, waits for them, and re-layouts: 3.1 us -> 1.47 us
    pallas_call x1, Pallas kernels: 63.9 us -> 53.2 us  [fused(): pl.pallas_call(functools.partial(kernel, n, inner, maxp), out_shape=jax.S...]
    pad x1 -> x0, local copies, waits for them, and re-layouts: 1.62 us -> none  [fused(): q_flat = jnp.pad(q_blocks, ((0, 0), (0, 0), (0, mp - maxp)))]
where the time goes in v2:
time: 54.8 us; the launch traced here: 54.7 us
  Pallas kernels  53.2 us (97%)
  local copies, waits for them, and re-layouts  1.47 us (3%)
    pallas_call x1, Pallas kernels, fused(): pl.pallas_call(functools.partial(kernel, n, inner, maxp), out_shape=jax.S...  53.2 us
    unnamed x1, local copies, waits for them, and re-layouts  1.47 us

profile of v2, /device:TPU:0, one launch (start us, length us, event | category | flops | bytes accessed | tf_op | source)
XLA Modules:
  0.0 54.7 jit_solution(10948760061575750826)
XLA Ops:
  0.0 53.2 %shard_map.55 = f32[16,1024]{1,0:T(8,128)} custom-call(bf16[4096,1024]{1,0:T(8,128)(2,1)} %psi_h.1, bf16[4096,128]{1,0:T(8,128)(2,1)} %trial_h.1, bf16[4096,1536]{1,0:T(8,128)(2,1)} %beta_h.1, f32[18,18,128]{2,1,0:T(8,128)} %bitcast.4, s32[1,128]{1,0:T(1,128)} %bitcast.5), custom_call_target="tpu_custom_call" | custom-call | tf_op jit(solution)/shard_map/pallas_call | solution.py:412
  53.2 1.5 %copy.7 = f32[1024,16]{0,1:T(8,128)} copy(f32[1024,16]{0,1:T(8,128)} %bitcast.3) | data formatting | bytes 131072

commit v3 on v2

v3 whole, which is shorter than its diff:
```python
import functools

import jax
import jax.numpy as jnp
from jax import lax
from jax.experimental import pallas as pl
from jax.experimental.pallas import tpu as pltpu
from jax.sharding import PartitionSpec as P

MESH = pl.DeviceIdType.MESH
precise = lax.Precision.HIGHEST
F32, BF16, I16 = jnp.float32, jnp.bfloat16, jnp.int16
LEVELS, TINY = 32767.0, 1e-30


def contract(left, right, precision=None):
    return lax.dot_general(
        left, right, (((0,), (0,)), ((), ())), precision=precision, preferred_element_type=F32
    )


def split2(x):
    hi = x.astype(BF16)
    return hi, (x - hi.astype(F32)).astype(BF16)


def encode(x):
    top = jnp.maximum(jnp.max(jnp.abs(x), keepdims=True), TINY)
    return jnp.round(x * (LEVELS / top)).astype(jnp.int32).astype(I16), top * (1.0 / LEVELS)


def decode(code, scale):
    return code.astype(jnp.int32).astype(F32) * scale


def kernel(
    n, maxp, psi_h, trial_h, beta_h, q_h, cnt_h, out_ref,
    psi_v, beta_v, trial_v, q_v, cnt_v, beta_t0, beta_t1, beta_t2, trial_t, q_parts, qd, g_hi, g_lo, w_hi, w_lo,
    proj, code1, scale1, in1, in1s, mid1, code1b, scale1b, end1, end1s,
    wall, walls, fin, code3, scale3, in3, in3s, mid3, code3b, scale3b, end3, end3s,
    q_sem, trial_sem, beta_sem, psi_sem, xs, xr, sent, recv1, recv1b, recv2, recv2b, recv2c,
    recv3, recv3b,
):
    me = lax.axis_index("ga")
    band = lax.axis_index("band")
    bit = [lax.rem(lax.div(me, 1 << p), 2) for p in range(4)]
    routes = (((1, 0), (3, 2)), ((2, 1), (3, 0)), ((2, 0), (3, 1)))
    peers = (3, 2, 1)

    def toggled(pair, d):
        return {p: lax.rem(bit[p] + (d >> k & 1), 2) for k, p in enumerate(pair[::-1])}

    def device(pair, d):
        there = sum((v - bit[p]) * (1 << p) for p, v in toggled(pair, d).items())
        return dict(device_id=(me + there, band), device_id_type=MESH)

    def pick(pair, d):
        bits = toggled(pair, d)
        return tuple(bits.get(p, slice(None)) for p in (3, 2, 1, 0))

    def cell(pair, d):
        bits = toggled(pair, d)
        return tuple(bits[p] for p in pair)

    partner = dict(device_id=(me, 1 - band), device_id_type=MESH)

    g, cols = trial_v.shape
    p_size = beta_v.shape[1]
    nbands = psi_v.shape[1]
    natom = cnt_v.shape[1]
    mp = q_parts.shape[1] // maxp
    r1 = cols // n
    r2 = out_ref.shape[0]
    beta_chunks = beta_sem.shape[0]
    bw = p_size // beta_chunks
    psi_chunks = psi_sem.shape[0]
    pw = nbands // psi_chunks
    sw = 512
    beta_t = (beta_t0, beta_t1, beta_t2)

    def aligned(i, size):
        return pl.ds(i * size if isinstance(i, int) else pl.multiple_of(i * size, size), size)

    def beta_copy(c):
        at = (slice(None), pl.ds(c * bw, bw))
        return pltpu.make_async_copy(beta_h.at[at], beta_v.at[at], beta_sem.at[c])

    def psi_copy(c):
        at = (slice(None), pl.ds(c * pw, pw))
        return pltpu.make_async_copy(psi_h.at[at], psi_v.at[at], psi_sem.at[c])

    q_copy = pltpu.make_async_copy(q_h, q_v, q_sem.at[0])
    cnt_copy = pltpu.make_async_copy(cnt_h, cnt_v, q_sem.at[1])
    trial_copy = pltpu.make_async_copy(trial_h, trial_v, trial_sem)
    q_copy.start()
    cnt_copy.start()
    trial_copy.start()
    beta_copy(0).start()

    barrier = pltpu.get_barrier_semaphore()

    met = [(pair, d) for pair in routes[0] for d in peers]
    met += [(pair, 3) for route in routes[1:] for pair in route]
    for pair, d in met:
        pl.semaphore_signal(barrier, inc=1, **device(pair, d))
    pl.semaphore_signal(barrier, inc=1, **partner)

    def send(stage, src, src_s, dst, dst_s, recv, to):
        for i, (a, b) in enumerate(((src, dst), (src_s, dst_s))):
            pltpu.make_async_remote_copy(
                src_ref=a, dst_ref=b, send_sem=sent.at[stage, i], recv_sem=recv.at[i], **to
            ).start()

    def landed(ref, ref_s, recv):
        for i, a in enumerate((ref, ref_s)):
            pltpu.make_async_remote_copy(
                src_ref=a, dst_ref=a, send_sem=sent.at[0, i], recv_sem=recv.at[i], **partner
            ).wait_recv()

    def left(stage, ref, ref_s):
        for i, a in enumerate((ref, ref_s)):
            pltpu.make_async_remote_copy(
                src_ref=a, dst_ref=a, send_sem=sent.at[stage, i], recv_sem=recv1.at[0, i], **partner
            ).wait_send()

    others = pl.ds(1, 3)

    def middle1(c):
        near, late = routes[c % 3]
        at = pl.ds(c * bw, bw)
        landed(in1.at[others, :, :, :, at], in1s.at[c, others], recv1.at[c])
        total = proj[pick(near, 0) + (slice(None), at)].reshape(4 * r1, bw)
        for d in peers:
            total += decode(in1[d, :, :, :, at].reshape(4 * r1, bw), in1s[c, d][:, :1])
        code, scale = encode(total)
        scale1b[c] = jnp.broadcast_to(scale, (1, 128))
        code1b[:, :, :, at] = code.reshape(2, 2, r1, bw)
        mid1[:, :, :, at] = total.reshape(2, 2, r1, bw)
        for d in peers:
            send(
                1, code1b.at[cell(late, d) + (slice(None), at)], scale1b.at[c],
                end1.at[d, :, at], end1s.at[c, d], recv1b.at[c], device(late, d),
            )

    with jax.named_scope("q_wait"):
        q_copy.wait()
        cnt_copy.wait()
    beta_copy(1).start()
    with jax.named_scope("diag"):
        cnt = cnt_v[...].astype(F32)
        row = lax.broadcasted_iota(jnp.int32, (natom, natom), 0)
        col = lax.broadcasted_iota(jnp.int32, (natom, natom), 1)
        offs = jnp.sum(jnp.where(col < row, cnt, 0.0), axis=1, keepdims=True)
        own = jnp.sum(jnp.where(col == row, cnt, 0.0), axis=1, keepdims=True)
        q_parts[...] = jnp.zeros_like(q_parts)
        for i in range(maxp):
            q = q_v[i]
            q_hi = q.astype(BF16)
            rest = q - q_hi.astype(F32)
            q_mid = rest.astype(BF16)
            at = slice(i * mp, i * mp + maxp)
            q_parts[0, at] = q_hi
            q_parts[1, at] = q_mid
            q_parts[2, at] = (rest - q_mid.astype(F32)).astype(BF16)

        def diagonals(c, _):
            lanes = 256
            nd = qd.shape[0]
            ids = (c * lanes + lax.broadcasted_iota(jnp.int32, (natom, lanes), 1)).astype(F32)
            owns = (offs <= ids) & (ids < offs + own)
            pos = jnp.sum(jnp.where(owns, ids - offs, 0.0), axis=0, keepdims=True)
            count = jnp.sum(
                jnp.where(owns, jnp.broadcast_to(own, owns.shape), 0.0), axis=0, keepdims=True
            )
            pick = jnp.where(owns, 1.0, 0.0).astype(BF16)
            flat = jnp.dot(q_parts[0], pick, preferred_element_type=F32)
            flat += jnp.dot(q_parts[1], pick, preferred_element_type=F32)
            flat += jnp.dot(q_parts[2], pick, preferred_element_type=F32)
            q_row = jnp.zeros((mp, lanes), F32)
            for i in range(maxp):
                q_row += jnp.where(pos == float(i), flat[i * mp : (i + 1) * mp], 0.0)
            at = pos + lax.broadcasted_iota(jnp.int32, (nd, lanes), 0).astype(F32) - float(maxp - 1)
            entries = jnp.zeros((nd, lanes), F32)
            for j in range(maxp):
                entries += jnp.where(at == float(j), q_row[j : j + 1], 0.0)
            qd[:, aligned(c, lanes)] = jnp.where(at < count, entries, 0.0)
            return 0

        for c in range(p_size // 256):
            diagonals(c, 0)
            if c == 2:
                beta_copy(2).start()

    with jax.named_scope("trial_wait"):
        trial_copy.wait()
    psi_copy(0).start()

    def turn(k, _):
        trial_t[aligned(band, cols), aligned(k, sw)] = trial_v[aligned(k, sw), :].T
        return 0

    with jax.named_scope("turn"):
        for k in range(g // sw):
            turn(k, 0)

    trial_x = pltpu.make_async_remote_copy(
        src_ref=trial_t.at[aligned(band, cols), :],
        dst_ref=trial_t.at[aligned(band, cols), :],
        send_sem=xs,
        recv_sem=xr,
        **partner,
    )

    for c in range(beta_chunks):
        with jax.named_scope(f"load_{c}"):
            beta_copy(c).wait()
        at = pl.ds(c * bw, bw)
        with jax.named_scope(f"p1_{c}"):
            part = jnp.dot(
                trial_t[aligned(band, cols), :], beta_v[:, at], preferred_element_type=F32
            )
            code, scale = encode(part)
            proj[:, :, :, :, :, at] = part.reshape(2, 2, 2, 2, r1, bw)
            code1[:, :, :, :, :, at] = code.reshape(2, 2, 2, 2, r1, bw)
            scale1[c] = jnp.broadcast_to(scale, (1, 128))
            if c == 0:
                with jax.named_scope("barrier"):
                    pl.semaphore_wait(barrier, len(met) + 1)
                trial_x.start()
            near = routes[c % 3][0]
            for d in peers:
                send(
                    0, code1.at[pick(near, d) + (slice(None), at)], scale1.at[c],
                    in1.at[d, :, :, :, at], in1s.at[c, d], recv1.at[c], device(near, d),
                )
        for k in ((1,), (2, 3), ())[c]:
            psi_copy(k).start()

    step = bw // psi_chunks

    def flip(c, k):
        if c < beta_chunks:
            part = pl.ds(pl.multiple_of(c * bw + k * step, step), step)
            beta_t[c][aligned(k, step), :] = beta_v[:, part].T

    def plain(lo, hi):
        def piece(k, _):
            psi_copy(k).wait()
            flip(0, k)
            got = jnp.dot(trial_t[...], psi_v[:, aligned(k, pw)], preferred_element_type=F32)
            fin[..., aligned(k, pw)] = got.reshape(2, 2, 2, 2, r2, pw)
            return 0

        with jax.named_scope(f"plain_{lo}"):
            lax.fori_loop(lo, hi, piece, 0)

    def bands(c, lo, hi, turns=1):
        def piece(k, _):
            for j in range(turns):
                flip(c + 1, k * turns + j)
            got = jnp.dot(beta_t[c][...], psi_v[:, aligned(k, pw)], preferred_element_type=F32)
            top, rest = split2(got)
            at = (pl.ds(c * bw, bw), aligned(k, pw))
            g_hi[at] = top
            g_lo[at] = rest
            return 0

        with jax.named_scope(f"bands_{c}_{lo}"):
            lax.fori_loop(lo, hi, piece, 0)

    with jax.named_scope("trial_x"):
        trial_x.wait()
    plain(0, 4)
    for c in range(beta_chunks):
        with jax.named_scope(f"mid1_{c}"):
            middle1(c)
    bands(0, 0, 4)

    with jax.named_scope("wait_z1"):
        for c in range(beta_chunks):
            landed(end1.at[others, :, pl.ds(c * bw, bw)], end1s.at[c, others], recv1b.at[c])

    with jax.named_scope("q_apply"):
        pieces = []
        for c in range(beta_chunks):
            at = pl.ds(c * bw, bw)
            piece = mid1[cell(routes[c % 3][1], 0) + (slice(None), at)]
            for d in peers:
                piece += decode(end1[d, :, at], end1s[c, d][:, :1])
            pieces.append(piece)
        x = jnp.concatenate(pieces, axis=1)
        acc = jnp.zeros_like(x)
        for d in range(2 * maxp - 1):
            shift = (maxp - 1 - d) % p_size
            moved = x if shift == 0 else pltpu.roll(x, shift, axis=1)
            acc += qd[d : d + 1, :] * moved
        code, scale = encode(acc)
        wall[(band,) + pick((3, 2), 0)[:2] + pick((1, 0), 0)[2:]] = code
        walls[(band,) + pick((3, 2), 0)[:2] + pick((1, 0), 0)[2:]] = jnp.broadcast_to(
            scale, (1, 128)
        )

    plane, line = routes[0]

    def share_w(stage, at, recv, to):
        a, b = wall.at[at], walls.at[at]
        send(stage, a, b, a, b, recv, to)

    def block(d):
        return (band,) + cell(line, d) + cell(plane, 0)

    def column(b, d):
        return (b,) + pick(plane, d)

    for d in peers:
        share_w(2, block(0), recv2.at[d - 1], device(line, d))
    for d in peers:
        share_w(3, block(0), recv2b.at[d - 1], device(plane, d))

    def relay(e):
        landed(wall.at[block(e)], walls.at[block(e)], recv2.at[e - 1])
        for d in peers:
            share_w(3, block(e), recv2b.at[d - 1], device(plane, d))

    def spread(b, d):
        y, x = cell(plane, d)
        for i in range(2):
            for k in range(2):
                at = (b, i, k, y, x)
                top, rest = split2(decode(wall[at], walls[at][:, :1]))
                w_hi[at] = top
                w_lo[at] = rest

    bands(1, 0, 2, 2)
    with jax.named_scope("ag_z1"):
        relay(1)
    bands(1, 2, 3, 0)
    with jax.named_scope("ag_z2"):
        relay(2)
    bands(1, 3, 4, 0)
    with jax.named_scope("ag_z3"):
        relay(3)
        share_w(4, column(band, 0), recv2c.at[0], partner)
    bands(2, 0, 4)

    with jax.named_scope("ag_xy"):
        for d in (1, 2, 3):
            landed(wall.at[column(band, d)], walls.at[column(band, d)], recv2b.at[d - 1])
            share_w(4, column(band, d), recv2c.at[d], partner)
    with jax.named_scope("spread_own"):
        for d in range(4):
            spread(band, d)
    with jax.named_scope("across"):
        for d in range(4):
            at = column(1 - band, d)
            landed(wall.at[at], walls.at[at], recv2c.at[d])
            spread(1 - band, d)

    def middle3(c):
        near, late = routes[c % 3]
        at = aligned(c, pw)
        landed(in3.at[others, :, :, :, at], in3s.at[c, others], recv3.at[c])
        total = fin[pick(near, 0) + (slice(None), at)].reshape(4 * r2, pw)
        for d in peers:
            total += decode(in3[d, :, :, :, at].reshape(4 * r2, pw), in3s[c, d][:, :1])
        code, scale = encode(total)
        scale3b[c] = jnp.broadcast_to(scale, (1, 128))
        code3b[:, :, :, at] = code.reshape(2, 2, r2, pw)
        mid3[:, :, :, at] = total.reshape(2, 2, r2, pw)
        for d in peers:
            send(
                6, code3b.at[cell(late, d) + (slice(None), at)], scale3b.at[c],
                end3.at[d, :, at], end3s.at[c, d], recv3b.at[c], device(late, d),
            )

    def product(c):
        at = aligned(c, pw)
        hi = w_hi[...].reshape(2 * cols, p_size)
        f = jnp.dot(hi, g_hi[:, at], preferred_element_type=F32)
        f += jnp.dot(hi, g_lo[:, at], preferred_element_type=F32)
        f += jnp.dot(w_lo[...].reshape(2 * cols, p_size), g_hi[:, at], preferred_element_type=F32)
        return f + fin[..., at].reshape(2 * cols, pw)

    def share(c, f):
        near = routes[c % 3][0]
        at = aligned(c, pw)
        code, scale = encode(f)
        scale3[c] = jnp.broadcast_to(scale, (1, 128))
        code3[..., at] = code.reshape(2, 2, 2, 2, r2, pw)
        fin[..., at] = f.reshape(2, 2, 2, 2, r2, pw)
        for d in peers:
            send(
                5, code3.at[pick(near, d) + (slice(None), at)], scale3.at[c],
                in3.at[d, :, :, :, at], in3s.at[c, d], recv3.at[c], device(near, d),
            )

    with jax.named_scope("share"):
        f = product(0)
        for c in range(psi_chunks):
            later = product(c + 1) if c + 1 < psi_chunks else None
            share(c, f)
            f = later
    for c in range(psi_chunks):
        with jax.named_scope(f"mid3_{c}"):
            middle3(c)

    with jax.named_scope("tail"):
        for c in range(psi_chunks):
            at = aligned(c, pw)
            landed(end3.at[others, :, at], end3s.at[c, others], recv3b.at[c])
            total = mid3[cell(routes[c % 3][1], 0) + (slice(None), at)]
            for d in peers:
                total += decode(end3[d, :, at], end3s[c, d][:, :1])
            out_ref[:, at] = total

    with jax.named_scope("drain"):
        three = pl.ds(0, 3)
        left(0, in1.at[others], in1s.at[:, three])
        left(1, end1.at[others], end1s.at[:, three])
        left(2, end1.at[others], end1s.at[0, three])
        left(3, in1.at[others], in3s.at[three])
        left(4, wall.at[0], walls.at[0])
        left(5, in3.at[others], in3s.at[:, three])
        left(6, end3.at[others], end3s.at[:, three])


def fused(n, blk, psi, trial, beta, q_blocks, atom_counts):
    g, cols = trial.shape
    nbands = psi.shape[1]
    p_size = beta.shape[1]
    natom, maxp = q_blocks.shape[:2]
    mp = -(-maxp // 8) * 8
    nd = -(-(2 * maxp - 1) // 8) * 8
    r1, r2 = cols // n, blk // n
    bc, pc = 3, 4
    dma = pltpu.SemaphoreType.DMA
    vm = pltpu.VMEM
    out = pl.pallas_call(
        functools.partial(kernel, n, maxp),
        out_shape=jax.ShapeDtypeStruct((r2, nbands), F32),
        in_specs=[pl.BlockSpec(memory_space=pl.ANY)] * 5,
        out_specs=pl.BlockSpec(memory_space=pltpu.VMEM),
        scratch_shapes=[
            vm((g, nbands), BF16),
            vm((g, p_size), BF16),
            vm((g, cols), BF16),
            vm((maxp, maxp, natom), F32),
            vm((1, natom), jnp.int32),
            vm((p_size // bc, g), BF16),
            vm((p_size // bc, g), BF16),
            vm((p_size // bc, g), BF16),
            vm((blk, g), BF16),
            vm((3, maxp * mp, natom), BF16),
            vm((nd, p_size), F32),
            vm((p_size, nbands), BF16),
            vm((p_size, nbands), BF16),
            vm((2, 2, 2, 2, 2, r1, p_size), BF16),
            vm((2, 2, 2, 2, 2, r1, p_size), BF16),
            vm((2, 2, 2, 2, r1, p_size), F32),
            vm((2, 2, 2, 2, r1, p_size), I16),
            vm((bc, 1, 128), F32),
            vm((4, 2, 2, r1, p_size), I16),
            vm((bc, 4, 1, 128), F32),
            vm((2, 2, r1, p_size), F32),
            vm((2, 2, r1, p_size), I16),
            vm((bc, 1, 128), F32),
            vm((4, r1, p_size), I16),
            vm((bc, 4, 1, 128), F32),
            vm((2, 2, 2, 2, 2, r1, p_size), I16),
            vm((2, 2, 2, 2, 2, 1, 128), F32),
            vm((2, 2, 2, 2, r2, nbands), F32),
            vm((2, 2, 2, 2, r2, nbands), I16),
            vm((pc, 1, 128), F32),
            vm((4, 2, 2, r2, nbands), I16),
            vm((pc, 4, 1, 128), F32),
            vm((2, 2, r2, nbands), F32),
            vm((2, 2, r2, nbands), I16),
            vm((pc, 1, 128), F32),
            vm((4, r2, nbands), I16),
            vm((pc, 4, 1, 128), F32),
            dma((2,)),
            dma,
            dma((bc,)),
            dma((pc,)),
            dma,
            dma,
            dma((7, 2)),
            dma((bc, 2)),
            dma((bc, 2)),
            dma((3, 2)),
            dma((3, 2)),
            dma((4, 2)),
            dma((pc, 2)),
            dma((pc, 2)),
        ],
        compiler_params=pltpu.CompilerParams(
            collective_id=0, has_side_effects=True, vmem_limit_bytes=62 * 1024 * 1024
        ),
    )(psi, trial, beta, q_blocks.transpose(1, 2, 0), atom_counts.reshape(1, natom))
    return out.T


def q_dense(atom_counts, q_blocks, p_size):
    offsets = jnp.cumsum(atom_counts, dtype=jnp.int32) - atom_counts
    natom, maxp = q_blocks.shape[:2]
    ids = jnp.arange(p_size, dtype=jnp.int32)
    owns = (offsets[None, :] <= ids[:, None]) & (ids[:, None] < (offsets + atom_counts)[None, :])
    pos = jnp.sum(jnp.where(owns, ids[:, None] - offsets[None, :], 0), axis=1)
    atom = jnp.sum(jnp.where(owns, jnp.arange(natom, dtype=jnp.int32)[None, :], 0), axis=1)
    flat = jnp.dot(owns.astype(F32), q_blocks.reshape(natom, maxp * maxp), precision=precise)
    place = pos[:, None] == jnp.arange(maxp, dtype=jnp.int32)[None, :]
    rows = jnp.sum(jnp.where(place[:, :, None], flat.reshape(p_size, maxp, maxp), 0.0), axis=1)
    entries = jnp.dot(rows, place.astype(F32).T, precision=precise)
    return jnp.where(atom[:, None] == atom[None, :], entries, 0.0)


def general(psi, trial, beta, q_blocks, atom_counts):
    own = lax.psum(contract(beta, trial), "ga")
    weighted = jnp.dot(q_dense(atom_counts, q_blocks, beta.shape[1]), own, precision=precise)
    w_hi, w_lo = split2(weighted)
    both = jnp.dot(beta, jnp.concatenate([w_hi, w_lo], axis=1), preferred_element_type=F32)
    cols = trial.shape[1]
    s = both[:, :cols] + both[:, cols:] + trial.astype(F32)
    s_hi, s_lo = split2(lax.all_gather(s, "band", axis=1, tiled=True))
    part = contract(psi, s_hi) + contract(psi, s_lo)
    return lax.psum_scatter(part, "ga", scatter_dimension=1, tiled=True)


def solution(mesh):
    n, bands = mesh.shape["ga"], mesh.shape["band"]

    def shards(psi, trial, beta, q_blocks, atom_counts):
        g, cols = trial.shape
        blk = cols * bands
        fits = (
            bands == 2
            and n == 16
            and cols % 128 == 0
            and cols % (8 * n) == 0
            and blk % (8 * n) == 0
            and g % 4096 == 0
            and beta.shape[1] % 768 == 0
            and psi.shape[1] % 512 == 0
            and q_blocks.shape[0] % 128 == 0
        )
        if fits:
            return fused(n, blk, psi, trial, beta, q_blocks, atom_counts)
        return general(psi, trial, beta, q_blocks, atom_counts)

    in_specs = (P("ga", "band"), P("ga", "band"), P("ga", None), P(), P())
    out_specs = P("band", "ga")
    return jax.shard_map(shards, mesh=mesh, in_specs=in_specs, out_specs=out_specs, check_vma=False)
```

time: 54.8 us -> 49.7 us (0.907)
  Pallas kernels: 53.2 us -> 48.1 us
    pallas_call x1, Pallas kernels: 53.2 us -> 48.1 us  [fused(): pl.pallas_call(functools.partial(kernel, n, maxp), out_shape=jax.ShapeDty...]
where the time goes in v3:
time: 49.7 us; the launch traced here: 49.6 us
  Pallas kernels  48.1 us (97%)
  local copies, waits for them, and re-layouts  1.47 us (3%)
    pallas_call x1, Pallas kernels, fused(): pl.pallas_call(functools.partial(kernel, n, maxp), out_shape=jax.ShapeDty...  48.1 us
    unnamed x1, local copies, waits for them, and re-layouts  1.47 us

profile of v3, /device:TPU:0, one launch (start us, length us, event | category | flops | bytes accessed | tf_op | source)
XLA Modules:
  0.0 49.6 jit_solution(3526641310472117294)
XLA Ops:
  0.0 48.1 %shard_map.55 = f32[16,1024]{1,0:T(8,128)} custom-call(bf16[4096,1024]{1,0:T(8,128)(2,1)} %psi_h.1, bf16[4096,128]{1,0:T(8,128)(2,1)} %trial_h.1, bf16[4096,1536]{1,0:T(8,128)(2,1)} %beta_h.1, f32[18,18,128]{2,1,0:T(8,128)} %bitcast.4, s32[1,128]{1,0:T(1,128)} %bitcast.5), custom_call_target="tpu_custom_call" | custom-call | tf_op jit(solution)/shard_map/pallas_call | solution.py:438
  48.1 1.5 %copy.7 = f32[1024,16]{0,1:T(8,128)} copy(f32[1024,16]{0,1:T(8,128)} %bitcast.3) | data formatting | bytes 131072

commit v4 on v3

--- a/solution.py
+++ b/solution.py
@@ -35,9 +35,9 @@
 
 def kernel(
     n, maxp, psi_h, trial_h, beta_h, q_h, cnt_h, out_ref,
-    psi_v, beta_v, trial_v, q_v, cnt_v, beta_t0, beta_t1, beta_t2, trial_t, q_parts, qd, g_hi, g_lo, w_hi, w_lo,
+    psi_v, beta_v, trial_v, q_v, cnt_v, lhs, beta_t, trial_t, q_parts, qd, g_hi, g_lo, w_hi, w_lo,
     proj, code1, scale1, in1, in1s, mid1, code1b, scale1b, end1, end1s,
-    wall, walls, fin, code3, scale3, in3, in3s, mid3, code3b, scale3b, end3, end3s,
+    wall, walls, fin, code3, scale3, in3, in3s, mid3, code3b, scale3b, end3, end3s, meter,
     q_sem, trial_sem, beta_sem, psi_sem, xs, xr, sent, recv1, recv1b, recv2, recv2b, recv2c,
     recv3, recv3b,
 ):
@@ -76,7 +76,6 @@
     psi_chunks = psi_sem.shape[0]
     pw = nbands // psi_chunks
     sw = 512
-    beta_t = (beta_t0, beta_t1, beta_t2)
 
     def aligned(i, size):
         return pl.ds(i * size if isinstance(i, int) else pl.multiple_of(i * size, size), size)
@@ -105,30 +104,32 @@
         pl.semaphore_signal(barrier, inc=1, **device(pair, d))
     pl.semaphore_signal(barrier, inc=1, **partner)
 
-    def send(stage, src, src_s, dst, dst_s, recv, to):
-        for i, (a, b) in enumerate(((src, dst), (src_s, dst_s))):
+    def send(src, src_s, dst, dst_s, recv, to):
+        for a, b in ((src, dst), (src_s, dst_s)):
             pltpu.make_async_remote_copy(
-                src_ref=a, dst_ref=b, send_sem=sent.at[stage, i], recv_sem=recv.at[i], **to
+                src_ref=a, dst_ref=b, send_sem=sent, recv_sem=recv, **to
             ).start()
 
-    def landed(ref, ref_s, recv):
-        for i, a in enumerate((ref, ref_s)):
-            pltpu.make_async_remote_copy(
-                src_ref=a, dst_ref=a, send_sem=sent.at[0, i], recv_sem=recv.at[i], **partner
-            ).wait_recv()
-
-    def left(stage, ref, ref_s):
-        for i, a in enumerate((ref, ref_s)):
-            pltpu.make_async_remote_copy(
-                src_ref=a, dst_ref=a, send_sem=sent.at[stage, i], recv_sem=recv1.at[0, i], **partner
-            ).wait_send()
-
-    others = pl.ds(1, 3)
+    def size(values, copies):
+        return copies * (2 * values + 4 * 128) // (4 * 128)
+
+    def counted(rows, recv):
+        a = meter.at[pl.ds(0, rows)]
+        return pltpu.make_async_remote_copy(
+            src_ref=a, dst_ref=a, send_sem=sent, recv_sem=recv, **partner
+        )
+
+    def landed(rows, recv):
+        counted(rows, recv).wait_recv()
+
+    near1, late1 = size(4 * r1 * bw, 3), size(r1 * bw, 3)
+    near3, late3 = size(4 * r2 * pw, 3), size(r2 * pw, 3)
+    one = size(r1 * p_size, 1)
 
     def middle1(c):
         near, late = routes[c % 3]
         at = pl.ds(c * bw, bw)
-        landed(in1.at[others, :, :, :, at], in1s.at[c, others], recv1.at[c])
+        landed(near1, recv1.at[c])
         total = proj[pick(near, 0) + (slice(None), at)].reshape(4 * r1, bw)
         for d in peers:
             total += decode(in1[d, :, :, :, at].reshape(4 * r1, bw), in1s[c, d][:, :1])
@@ -138,7 +139,7 @@
         mid1[:, :, :, at] = total.reshape(2, 2, r1, bw)
         for d in peers:
             send(
-                1, code1b.at[cell(late, d) + (slice(None), at)], scale1b.at[c],
+                code1b.at[cell(late, d) + (slice(None), at)], scale1b.at[c],
                 end1.at[d, :, at], end1s.at[c, d], recv1b.at[c], device(late, d),
             )
 
@@ -156,12 +157,9 @@
         for i in range(maxp):
             q = q_v[i]
             q_hi = q.astype(BF16)
-            rest = q - q_hi.astype(F32)
-            q_mid = rest.astype(BF16)
             at = slice(i * mp, i * mp + maxp)
             q_parts[0, at] = q_hi
-            q_parts[1, at] = q_mid
-            q_parts[2, at] = (rest - q_mid.astype(F32)).astype(BF16)
+            q_parts[1, at] = (q - q_hi.astype(F32)).astype(BF16)
 
         def diagonals(c, _):
             lanes = 256
@@ -175,7 +173,6 @@
             pick = jnp.where(owns, 1.0, 0.0).astype(BF16)
             flat = jnp.dot(q_parts[0], pick, preferred_element_type=F32)
             flat += jnp.dot(q_parts[1], pick, preferred_element_type=F32)
-            flat += jnp.dot(q_parts[2], pick, preferred_element_type=F32)
             q_row = jnp.zeros((mp, lanes), F32)
             for i in range(maxp):
                 q_row += jnp.where(pos == float(i), flat[i * mp : (i + 1) * mp], 0.0)
@@ -195,8 +192,12 @@
         trial_copy.wait()
     psi_copy(0).start()
 
+    mine_t = pl.ds(pl.multiple_of(bw + band * cols, cols), cols)
+
     def turn(k, _):
-        trial_t[aligned(band, cols), aligned(k, sw)] = trial_v[aligned(k, sw), :].T
+        own = trial_v[aligned(k, sw), :].T
+        trial_t[:, aligned(k, sw)] = own
+        lhs[mine_t, aligned(k, sw)] = own
         return 0
 
     with jax.named_scope("turn"):
@@ -204,162 +205,176 @@
             turn(k, 0)
 
     trial_x = pltpu.make_async_remote_copy(
-        src_ref=trial_t.at[aligned(band, cols), :],
-        dst_ref=trial_t.at[aligned(band, cols), :],
+        src_ref=trial_t,
+        dst_ref=lhs.at[mine_t, :],
         send_sem=xs,
         recv_sem=xr,
         **partner,
     )
 
-    for c in range(beta_chunks):
-        with jax.named_scope(f"load_{c}"):
+    def flip(to, first, k, rows):
+        part = pl.ds(pl.multiple_of(first + k * rows, rows), rows)
+        to[aligned(k, rows), :] = beta_v[:, part].T
+
+    def project(c, _):
+        with jax.named_scope("load"):
             beta_copy(c).wait()
-        at = pl.ds(c * bw, bw)
-        with jax.named_scope(f"p1_{c}"):
-            part = jnp.dot(
-                trial_t[aligned(band, cols), :], beta_v[:, at], preferred_element_type=F32
-            )
+        at = aligned(c, bw)
+        with jax.named_scope("p1"):
+            part = jnp.dot(trial_t[...], beta_v[:, at], preferred_element_type=F32)
+            flip(lhs, 0, jnp.minimum(c, 1), bw // 2)
             code, scale = encode(part)
             proj[:, :, :, :, :, at] = part.reshape(2, 2, 2, 2, r1, bw)
             code1[:, :, :, :, :, at] = code.reshape(2, 2, 2, 2, r1, bw)
             scale1[c] = jnp.broadcast_to(scale, (1, 128))
-            if c == 0:
-                with jax.named_scope("barrier"):
-                    pl.semaphore_wait(barrier, len(met) + 1)
-                trial_x.start()
-            near = routes[c % 3][0]
-            for d in peers:
-                send(
-                    0, code1.at[pick(near, d) + (slice(None), at)], scale1.at[c],
-                    in1.at[d, :, :, :, at], in1s.at[c, d], recv1.at[c], device(near, d),
-                )
-        for k in ((1,), (2, 3), ())[c]:
-            psi_copy(k).start()
-
-    step = bw // psi_chunks
-
-    def flip(c, k):
-        if c < beta_chunks:
-            part = pl.ds(pl.multiple_of(c * bw + k * step, step), step)
-            beta_t[c][aligned(k, step), :] = beta_v[:, part].T
-
-    def plain(lo, hi):
-        def piece(k, _):
-            psi_copy(k).wait()
-            flip(0, k)
-            got = jnp.dot(trial_t[...], psi_v[:, aligned(k, pw)], preferred_element_type=F32)
-            fin[..., aligned(k, pw)] = got.reshape(2, 2, 2, 2, r2, pw)
-            return 0
-
-        with jax.named_scope(f"plain_{lo}"):
-            lax.fori_loop(lo, hi, piece, 0)
-
-    def bands(c, lo, hi, turns=1):
-        def piece(k, _):
-            for j in range(turns):
-                flip(c + 1, k * turns + j)
-            got = jnp.dot(beta_t[c][...], psi_v[:, aligned(k, pw)], preferred_element_type=F32)
-            top, rest = split2(got)
-            at = (pl.ds(c * bw, bw), aligned(k, pw))
-            g_hi[at] = top
-            g_lo[at] = rest
-            return 0
-
-        with jax.named_scope(f"bands_{c}_{lo}"):
-            lax.fori_loop(lo, hi, piece, 0)
+
+        @pl.when(c == 0)
+        def _():
+            with jax.named_scope("barrier"):
+                pl.semaphore_wait(barrier, len(met) + 1)
+            trial_x.start()
+
+        for i in range(beta_chunks):
+            near = routes[i % 3][0]
+            now = pl.ds(i * bw, bw)
+
+            @pl.when(c == i)
+            def _():
+                for d in peers:
+                    send(
+                        code1.at[pick(near, d) + (slice(None), now)], scale1.at[i],
+                        in1.at[d, :, :, :, now], in1s.at[i, d], recv1.at[i], device(near, d),
+                    )
+                for k in ((1,), (2, 3), ())[i]:
+                    psi_copy(k).start()
+
+        return 0
+
+    lax.fori_loop(0, beta_chunks, project, 0)
+
+    def keep(got, first, k):
+        top, rest = split2(got)
+        at = (aligned(first, bw), aligned(k, pw))
+        g_hi[at] = top
+        g_lo[at] = rest
 
     with jax.named_scope("trial_x"):
         trial_x.wait()
-    plain(0, 4)
-    for c in range(beta_chunks):
-        with jax.named_scope(f"mid1_{c}"):
-            middle1(c)
-    bands(0, 0, 4)
-
-    with jax.named_scope("wait_z1"):
-        for c in range(beta_chunks):
-            landed(end1.at[others, :, pl.ds(c * bw, bw)], end1s.at[c, others], recv1b.at[c])
-
-    with jax.named_scope("q_apply"):
-        pieces = []
-        for c in range(beta_chunks):
-            at = pl.ds(c * bw, bw)
-            piece = mid1[cell(routes[c % 3][1], 0) + (slice(None), at)]
-            for d in peers:
-                piece += decode(end1[d, :, at], end1s[c, d][:, :1])
-            pieces.append(piece)
-        x = jnp.concatenate(pieces, axis=1)
-        acc = jnp.zeros_like(x)
-        for d in range(2 * maxp - 1):
-            shift = (maxp - 1 - d) % p_size
-            moved = x if shift == 0 else pltpu.roll(x, shift, axis=1)
-            acc += qd[d : d + 1, :] * moved
-        code, scale = encode(acc)
-        wall[(band,) + pick((3, 2), 0)[:2] + pick((1, 0), 0)[2:]] = code
-        walls[(band,) + pick((3, 2), 0)[:2] + pick((1, 0), 0)[2:]] = jnp.broadcast_to(
-            scale, (1, 128)
-        )
+
+    def early(k, _):
+        @pl.when(k == 2)
+        def _():
+            for c in range(beta_chunks):
+                with jax.named_scope(f"mid1_{c}"):
+                    middle1(c)
+
+        with jax.named_scope("psi_wait"):
+            psi_copy(k).wait()
+        with jax.named_scope("bands_0"):
+            at = aligned(k, pw)
+            flip(beta_t, bw, k, 2 * bw // psi_chunks)
+            got = jnp.dot(lhs[...], psi_v[:, at], preferred_element_type=F32)
+            keep(got[:bw], 0, k)
+            fin[..., at] = got[bw:].reshape(2, 2, 2, 2, r2, pw)
+        return 0
+
+    lax.fori_loop(0, psi_chunks, early, 0)
 
     plane, line = routes[0]
 
-    def share_w(stage, at, recv, to):
+    def share_w(at, recv, to):
         a, b = wall.at[at], walls.at[at]
-        send(stage, a, b, a, b, recv, to)
+        send(a, b, a, b, recv, to)
 
     def block(d):
         return (band,) + cell(line, d) + cell(plane, 0)
 
-    def column(b, d):
-        return (b,) + pick(plane, d)
-
-    for d in peers:
-        share_w(2, block(0), recv2.at[d - 1], device(line, d))
-    for d in peers:
-        share_w(3, block(0), recv2b.at[d - 1], device(plane, d))
+    def weigh():
+        with jax.named_scope("wait_z1"):
+            for c in range(beta_chunks):
+                landed(late1, recv1b.at[c])
+
+        with jax.named_scope("q_apply"):
+            pieces = []
+            for c in range(beta_chunks):
+                at = pl.ds(c * bw, bw)
+                piece = mid1[cell(routes[c % 3][1], 0) + (slice(None), at)]
+                for d in peers:
+                    piece += decode(end1[d, :, at], end1s[c, d][:, :1])
+                pieces.append(piece)
+            x = jnp.concatenate(pieces, axis=1)
+            acc = jnp.zeros_like(x)
+            for d in range(2 * maxp - 1):
+                shift = (maxp - 1 - d) % p_size
+                moved = x if shift == 0 else pltpu.roll(x, shift, axis=1)
+                acc += qd[d : d + 1, :] * moved
+            code, scale = encode(acc)
+            wall[(band,) + pick((3, 2), 0)[:2] + pick((1, 0), 0)[2:]] = code
+            walls[(band,) + pick((3, 2), 0)[:2] + pick((1, 0), 0)[2:]] = jnp.broadcast_to(
+                scale, (1, 128)
+            )
+        for d in peers:
+            share_w(block(0), recv2.at[d - 1], device(line, d))
+        for d in peers:
+            share_w(block(0), recv2b.at[0], device(plane, d))
 
     def relay(e):
-        landed(wall.at[block(e)], walls.at[block(e)], recv2.at[e - 1])
-        for d in peers:
-            share_w(3, block(e), recv2b.at[d - 1], device(plane, d))
-
-    def spread(b, d):
-        y, x = cell(plane, d)
-        for i in range(2):
-            for k in range(2):
-                at = (b, i, k, y, x)
-                top, rest = split2(decode(wall[at], walls[at][:, :1]))
-                w_hi[at] = top
-                w_lo[at] = rest
-
-    bands(1, 0, 2, 2)
-    with jax.named_scope("ag_z1"):
-        relay(1)
-    bands(1, 2, 3, 0)
-    with jax.named_scope("ag_z2"):
-        relay(2)
-    bands(1, 3, 4, 0)
-    with jax.named_scope("ag_z3"):
-        relay(3)
-        share_w(4, column(band, 0), recv2c.at[0], partner)
-    bands(2, 0, 4)
+        landed(one, recv2.at[e - 1])
+        for d in peers:
+            share_w(block(e), recv2b.at[e], device(plane, d))
+
+    def across(e):
+        landed(3 * one, recv2b.at[e])
+        row = (band,) + cell(line, e)
+        a, b = wall.at[row], walls.at[row]
+        send(a, b, a, b, recv2c.at[e], partner)
+
+    def spread(b, e):
+        high, low = cell(line, e)
+        values = decode(wall[b, high, low], walls[b, high, low][..., :1])
+        top, rest = split2(values.reshape(4 * r1, p_size))
+        at = aligned(b * 4 + high * 2 + low, 4 * r1)
+        w_hi[at, :] = top
+        w_lo[at, :] = rest
+
+    def late(u, _):
+        for when, steps in (
+            (1, (weigh,)),
+            (3, (functools.partial(relay, 1),)),
+            (4, (functools.partial(relay, 2),)),
+            (5, (functools.partial(relay, 3), functools.partial(across, 0))),
+            (6, (functools.partial(across, 1),)),
+            (7, (functools.partial(across, 2),)),
+        ):
+
+            @pl.when(u == when)
+            def _():
+                with jax.named_scope(f"service_{when}"):
+                    for step in steps:
+                        step()
+
+        with jax.named_scope("bands_1"):
+            c, k = lax.div(u, psi_chunks), lax.rem(u, psi_chunks)
+            rows = beta_t[aligned(c, bw), :]
+            keep(jnp.dot(rows, psi_v[:, aligned(k, pw)], preferred_element_type=F32), c + 1, k)
+        return 0
+
+    lax.fori_loop(0, (beta_chunks - 1) * psi_chunks, late, 0)
 
     with jax.named_scope("ag_xy"):
-        for d in (1, 2, 3):
-            landed(wall.at[column(band, d)], walls.at[column(band, d)], recv2b.at[d - 1])
-            share_w(4, column(band, d), recv2c.at[d], partner)
+        across(3)
     with jax.named_scope("spread_own"):
-        for d in range(4):
-            spread(band, d)
+        for e in range(4):
+            spread(band, e)
     with jax.named_scope("across"):
-        for d in range(4):
-            at = column(1 - band, d)
-            landed(wall.at[at], walls.at[at], recv2c.at[d])
-            spread(1 - band, d)
+        for e in range(4):
+            landed(4 * one, recv2c.at[e])
+            spread(1 - band, e)
 
     def middle3(c):
         near, late = routes[c % 3]
         at = aligned(c, pw)
-        landed(in3.at[others, :, :, :, at], in3s.at[c, others], recv3.at[c])
+        landed(near3, recv3.at[c])
         total = fin[pick(near, 0) + (slice(None), at)].reshape(4 * r2, pw)
         for d in peers:
             total += decode(in3[d, :, :, :, at].reshape(4 * r2, pw), in3s[c, d][:, :1])
@@ -369,16 +384,15 @@
         mid3[:, :, :, at] = total.reshape(2, 2, r2, pw)
         for d in peers:
             send(
-                6, code3b.at[cell(late, d) + (slice(None), at)], scale3b.at[c],
+                code3b.at[cell(late, d) + (slice(None), at)], scale3b.at[c],
                 end3.at[d, :, at], end3s.at[c, d], recv3b.at[c], device(late, d),
             )
 
     def product(c):
         at = aligned(c, pw)
-        hi = w_hi[...].reshape(2 * cols, p_size)
-        f = jnp.dot(hi, g_hi[:, at], preferred_element_type=F32)
-        f += jnp.dot(hi, g_lo[:, at], preferred_element_type=F32)
-        f += jnp.dot(w_lo[...].reshape(2 * cols, p_size), g_hi[:, at], preferred_element_type=F32)
+        f = jnp.dot(w_hi[...], g_hi[:, at], preferred_element_type=F32)
+        f += jnp.dot(w_hi[...], g_lo[:, at], preferred_element_type=F32)
+        f += jnp.dot(w_lo[...], g_hi[:, at], preferred_element_type=F32)
         return f + fin[..., at].reshape(2 * cols, pw)
 
     def share(c, f):
@@ -390,7 +404,7 @@
         fin[..., at] = f.reshape(2, 2, 2, 2, r2, pw)
         for d in peers:
             send(
-                5, code3.at[pick(near, d) + (slice(None), at)], scale3.at[c],
+                code3.at[pick(near, d) + (slice(None), at)], scale3.at[c],
                 in3.at[d, :, :, :, at], in3s.at[c, d], recv3.at[c], device(near, d),
             )
 
@@ -407,21 +421,15 @@
     with jax.named_scope("tail"):
         for c in range(psi_chunks):
             at = aligned(c, pw)
-            landed(end3.at[others, :, at], end3s.at[c, others], recv3b.at[c])
+            landed(late3, recv3b.at[c])
             total = mid3[cell(routes[c % 3][1], 0) + (slice(None), at)]
             for d in peers:
                 total += decode(end3[d, :, at], end3s[c, d][:, :1])
             out_ref[:, at] = total
 
     with jax.named_scope("drain"):
-        three = pl.ds(0, 3)
-        left(0, in1.at[others], in1s.at[:, three])
-        left(1, end1.at[others], end1s.at[:, three])
-        left(2, end1.at[others], end1s.at[0, three])
-        left(3, in1.at[others], in3s.at[three])
-        left(4, wall.at[0], walls.at[0])
-        left(5, in3.at[others], in3s.at[:, three])
-        left(6, end3.at[others], end3s.at[:, three])
+        total = beta_chunks * (near1 + late1) + psi_chunks * (near3 + late3) + 31 * one
+        counted(total, recv1.at[0]).wait_send()
 
 
 def fused(n, blk, psi, trial, beta, q_blocks, atom_counts):
@@ -433,6 +441,7 @@
     nd = -(-(2 * maxp - 1) // 8) * 8
     r1, r2 = cols // n, blk // n
     bc, pc = 3, 4
+    meter = (2 * (15 * (cols * p_size + blk * nbands) // 16) + 2 * 16 * cols * p_size) // 512 + 256
     dma = pltpu.SemaphoreType.DMA
     vm = pltpu.VMEM
     out = pl.pallas_call(
@@ -446,16 +455,15 @@
             vm((g, cols), BF16),
             vm((maxp, maxp, natom), F32),
             vm((1, natom), jnp.int32),
-            vm((p_size // bc, g), BF16),
-            vm((p_size // bc, g), BF16),
-            vm((p_size // bc, g), BF16),
-            vm((blk, g), BF16),
-            vm((3, maxp * mp, natom), BF16),
+            vm((p_size // bc + blk, g), BF16),
+            vm((p_size - p_size // bc, g), BF16),
+            vm((cols, g), BF16),
+            vm((2, maxp * mp, natom), BF16),
             vm((nd, p_size), F32),
             vm((p_size, nbands), BF16),
             vm((p_size, nbands), BF16),
-            vm((2, 2, 2, 2, 2, r1, p_size), BF16),
-            vm((2, 2, 2, 2, 2, r1, p_size), BF16),
+            vm((blk, p_size), BF16),
+            vm((blk, p_size), BF16),
             vm((2, 2, 2, 2, r1, p_size), F32),
             vm((2, 2, 2, 2, r1, p_size), I16),
             vm((bc, 1, 128), F32),
@@ -478,20 +486,21 @@
             vm((pc, 1, 128), F32),
             vm((4, r2, nbands), I16),
             vm((pc, 4, 1, 128), F32),
+            vm((meter, 1, 128), F32),
             dma((2,)),
             dma,
             dma((bc,)),
             dma((pc,)),
             dma,
             dma,
-            dma((7, 2)),
-            dma((bc, 2)),
-            dma((bc, 2)),
-            dma((3, 2)),
-            dma((3, 2)),
-            dma((4, 2)),
-            dma((pc, 2)),
-            dma((pc, 2)),
+            dma,
+            dma((bc,)),
+            dma((bc,)),
+            dma((3,)),
+            dma((4,)),
+            dma((4,)),
+            dma((pc,)),
+            dma((pc,)),
         ],
         compiler_params=pltpu.CompilerParams(
             collective_id=0, has_side_effects=True, vmem_limit_bytes=62 * 1024 * 1024

time: 49.7 us -> 46.6 us (0.938)
  Pallas kernels: 48.1 us -> 44.9 us
    pallas_call x1, Pallas kernels: 48.1 us -> 44.9 us  [fused(): pl.pallas_call(functools.partial(kernel, n, maxp), out_shape=jax.ShapeDty...]
where the time goes in v4:
time: 46.6 us; the launch traced here: 46.4 us
  Pallas kernels  44.9 us (96%)
  local copies, waits for them, and re-layouts  1.47 us (3%)
    pallas_call x1, Pallas kernels, fused(): pl.pallas_call(functools.partial(kernel, n, maxp), out_shape=jax.ShapeDty...  44.9 us
    unnamed x1, local copies, waits for them, and re-layouts  1.47 us

profile of v4, /device:TPU:0, one launch (start us, length us, event | category | flops | bytes accessed | tf_op | source)
XLA Modules:
  0.0 46.4 jit_solution(1634486347561888494)
XLA Ops:
  0.0 44.9 %shard_map.55 = f32[16,1024]{1,0:T(8,128)} custom-call(bf16[4096,1024]{1,0:T(8,128)(2,1)} %psi_h.1, bf16[4096,128]{1,0:T(8,128)(2,1)} %trial_h.1, bf16[4096,1536]{1,0:T(8,128)(2,1)} %beta_h.1, f32[18,18,128]{2,1,0:T(8,128)} %bitcast.4, s32[1,128]{1,0:T(1,128)} %bitcast.5), custom_call_target="tpu_custom_call" | custom-call | tf_op jit(solution)/shard_map/pallas_call | solution.py:447
  44.9 1.5 %copy.7 = f32[1024,16]{0,1:T(8,128)} copy(f32[1024,16]{0,1:T(8,128)} %bitcast.3) | data formatting | bytes 131072

commit v5 on v4

--- a/solution.py
+++ b/solution.py
@@ -24,8 +24,10 @@
     return hi, (x - hi.astype(F32)).astype(BF16)
 
 
-def encode(x):
-    top = jnp.maximum(jnp.max(jnp.abs(x), keepdims=True), TINY)
+def encode(x, top=None):
+    if top is None:
+        top = jnp.max(jnp.abs(x), axis=0, keepdims=True)
+    top = jnp.maximum(top, TINY)
     return jnp.round(x * (LEVELS / top)).astype(jnp.int32).astype(I16), top * (1.0 / LEVELS)
 
 
@@ -110,8 +112,8 @@
                 src_ref=a, dst_ref=b, send_sem=sent, recv_sem=recv, **to
             ).start()
 
-    def size(values, copies):
-        return copies * (2 * values + 4 * 128) // (4 * 128)
+    def size(values, lanes, copies):
+        return copies * (2 * values + 4 * lanes) // (4 * 128)
 
     def counted(rows, recv):
         a = meter.at[pl.ds(0, rows)]
@@ -122,9 +124,9 @@
     def landed(rows, recv):
         counted(rows, recv).wait_recv()
 
-    near1, late1 = size(4 * r1 * bw, 3), size(r1 * bw, 3)
-    near3, late3 = size(4 * r2 * pw, 3), size(r2 * pw, 3)
-    one = size(r1 * p_size, 1)
+    near1, late1 = size(4 * r1 * bw, bw, 3), size(r1 * bw, bw, 3)
+    near3, late3 = size(4 * r2 * pw, pw, 3), size(r2 * pw, pw, 3)
+    one = size(r1 * p_size, 128, 1)
 
     def middle1(c):
         near, late = routes[c % 3]
@@ -132,9 +134,9 @@
         landed(near1, recv1.at[c])
         total = proj[pick(near, 0) + (slice(None), at)].reshape(4 * r1, bw)
         for d in peers:
-            total += decode(in1[d, :, :, :, at].reshape(4 * r1, bw), in1s[c, d][:, :1])
+            total += decode(in1[d, :, :, :, at].reshape(4 * r1, bw), in1s[c, d])
         code, scale = encode(total)
-        scale1b[c] = jnp.broadcast_to(scale, (1, 128))
+        scale1b[c] = scale
         code1b[:, :, :, at] = code.reshape(2, 2, r1, bw)
         mid1[:, :, :, at] = total.reshape(2, 2, r1, bw)
         for d in peers:
@@ -175,11 +177,11 @@
             flat += jnp.dot(q_parts[1], pick, preferred_element_type=F32)
             q_row = jnp.zeros((mp, lanes), F32)
             for i in range(maxp):
-                q_row += jnp.where(pos == float(i), flat[i * mp : (i + 1) * mp], 0.0)
+                q_row = jnp.where(pos == float(i), flat[i * mp : (i + 1) * mp], q_row)
             at = pos + lax.broadcasted_iota(jnp.int32, (nd, lanes), 0).astype(F32) - float(maxp - 1)
             entries = jnp.zeros((nd, lanes), F32)
             for j in range(maxp):
-                entries += jnp.where(at == float(j), q_row[j : j + 1], 0.0)
+                entries = jnp.where(at == float(j), q_row[j : j + 1], entries)
             qd[:, aligned(c, lanes)] = jnp.where(at < count, entries, 0.0)
             return 0
 
@@ -226,7 +228,7 @@
             code, scale = encode(part)
             proj[:, :, :, :, :, at] = part.reshape(2, 2, 2, 2, r1, bw)
             code1[:, :, :, :, :, at] = code.reshape(2, 2, 2, 2, r1, bw)
-            scale1[c] = jnp.broadcast_to(scale, (1, 128))
+            scale1[c] = scale
 
         @pl.when(c == 0)
         def _():
@@ -300,7 +302,7 @@
                 at = pl.ds(c * bw, bw)
                 piece = mid1[cell(routes[c % 3][1], 0) + (slice(None), at)]
                 for d in peers:
-                    piece += decode(end1[d, :, at], end1s[c, d][:, :1])
+                    piece += decode(end1[d, :, at], end1s[c, d])
                 pieces.append(piece)
             x = jnp.concatenate(pieces, axis=1)
             acc = jnp.zeros_like(x)
@@ -308,11 +310,12 @@
                 shift = (maxp - 1 - d) % p_size
                 moved = x if shift == 0 else pltpu.roll(x, shift, axis=1)
                 acc += qd[d : d + 1, :] * moved
-            code, scale = encode(acc)
+            tiles = [acc[:, t : t + 128] for t in range(0, p_size, 128)]
+            top = functools.reduce(jnp.maximum, [jnp.abs(t) for t in tiles])
+            top = jnp.max(top, axis=0, keepdims=True)
+            code, scale = encode(acc, jnp.concatenate([top] * len(tiles), axis=1))
             wall[(band,) + pick((3, 2), 0)[:2] + pick((1, 0), 0)[2:]] = code
-            walls[(band,) + pick((3, 2), 0)[:2] + pick((1, 0), 0)[2:]] = jnp.broadcast_to(
-                scale, (1, 128)
-            )
+            walls[(band,) + pick((3, 2), 0)[:2] + pick((1, 0), 0)[2:]] = scale[:, :128]
         for d in peers:
             share_w(block(0), recv2.at[d - 1], device(line, d))
         for d in peers:
@@ -331,7 +334,8 @@
 
     def spread(b, e):
         high, low = cell(line, e)
-        values = decode(wall[b, high, low], walls[b, high, low][..., :1])
+        scale = jnp.concatenate([walls[b, high, low]] * (p_size // 128), axis=-1)
+        values = decode(wall[b, high, low], scale)
         top, rest = split2(values.reshape(4 * r1, p_size))
         at = aligned(b * 4 + high * 2 + low, 4 * r1)
         w_hi[at, :] = top
@@ -377,9 +381,9 @@
         landed(near3, recv3.at[c])
         total = fin[pick(near, 0) + (slice(None), at)].reshape(4 * r2, pw)
         for d in peers:
-            total += decode(in3[d, :, :, :, at].reshape(4 * r2, pw), in3s[c, d][:, :1])
+            total += decode(in3[d, :, :, :, at].reshape(4 * r2, pw), in3s[c, d])
         code, scale = encode(total)
-        scale3b[c] = jnp.broadcast_to(scale, (1, 128))
+        scale3b[c] = scale
         code3b[:, :, :, at] = code.reshape(2, 2, r2, pw)
         mid3[:, :, :, at] = total.reshape(2, 2, r2, pw)
         for d in peers:
@@ -399,7 +403,7 @@
         near = routes[c % 3][0]
         at = aligned(c, pw)
         code, scale = encode(f)
-        scale3[c] = jnp.broadcast_to(scale, (1, 128))
+        scale3[c] = scale
         code3[..., at] = code.reshape(2, 2, 2, 2, r2, pw)
         fin[..., at] = f.reshape(2, 2, 2, 2, r2, pw)
         for d in peers:
@@ -424,7 +428,7 @@
             landed(late3, recv3b.at[c])
             total = mid3[cell(routes[c % 3][1], 0) + (slice(None), at)]
             for d in peers:
-                total += decode(end3[d, :, at], end3s[c, d][:, :1])
+                total += decode(end3[d, :, at], end3s[c, d])
             out_ref[:, at] = total
 
     with jax.named_scope("drain"):
@@ -441,7 +445,7 @@
     nd = -(-(2 * maxp - 1) // 8) * 8
     r1, r2 = cols // n, blk // n
     bc, pc = 3, 4
-    meter = (2 * (15 * (cols * p_size + blk * nbands) // 16) + 2 * 16 * cols * p_size) // 512 + 256
+    meter = (2 * (15 * (cols * p_size + blk * nbands) // 16) + 2 * 16 * cols * p_size) // 512 + 1024
     dma = pltpu.SemaphoreType.DMA
     vm = pltpu.VMEM
     out = pl.pallas_call(
@@ -466,26 +470,26 @@
             vm((blk, p_size), BF16),
             vm((2, 2, 2, 2, r1, p_size), F32),
             vm((2, 2, 2, 2, r1, p_size), I16),
-            vm((bc, 1, 128), F32),
+            vm((bc, 1, p_size // bc), F32),
             vm((4, 2, 2, r1, p_size), I16),
-            vm((bc, 4, 1, 128), F32),
+            vm((bc, 4, 1, p_size // bc), F32),
             vm((2, 2, r1, p_size), F32),
             vm((2, 2, r1, p_size), I16),
-            vm((bc, 1, 128), F32),
+            vm((bc, 1, p_size // bc), F32),
             vm((4, r1, p_size), I16),
-            vm((bc, 4, 1, 128), F32),
+            vm((bc, 4, 1, p_size // bc), F32),
             vm((2, 2, 2, 2, 2, r1, p_size), I16),
             vm((2, 2, 2, 2, 2, 1, 128), F32),
             vm((2, 2, 2, 2, r2, nbands), F32),
             vm((2, 2, 2, 2, r2, nbands), I16),
-            vm((pc, 1, 128), F32),
+            vm((pc, 1, nbands // pc), F32),
             vm((4, 2, 2, r2, nbands), I16),
-            vm((pc, 4, 1, 128), F32),
+            vm((pc, 4, 1, nbands // pc), F32),
             vm((2, 2, r2, nbands), F32),
             vm((2, 2, r2, nbands), I16),
-            vm((pc, 1, 128), F32),
+            vm((pc, 1, nbands // pc), F32),
             vm((4, r2, nbands), I16),
-            vm((pc, 4, 1, 128), F32),
+            vm((pc, 4, 1, nbands // pc), F32),
             vm((meter, 1, 128), F32),
             dma((2,)),
             dma,

time: 46.6 us -> 45.3 us (0.972)
  Pallas kernels: 44.9 us -> 43.6 us
    pallas_call x1, Pallas kernels: 44.9 us -> 43.6 us  [fused(): pl.pallas_call(functools.partial(kernel, n, maxp), out_shape=jax.ShapeDty...]
where the time goes in v5:
time: 45.3 us; the launch traced here: 45.1 us
  Pallas kernels  43.6 us (96%)
  local copies, waits for them, and re-layouts  1.47 us (3%)
    pallas_call x1, Pallas kernels, fused(): pl.pallas_call(functools.partial(kernel, n, maxp), out_shape=jax.ShapeDty...  43.6 us
    unnamed x1, local copies, waits for them, and re-layouts  1.47 us

profile of v5, /device:TPU:0, one launch (start us, length us, event | category | flops | bytes accessed | tf_op | source)
XLA Modules:
  0.0 45.1 jit_solution(16693560189897540445)
XLA Ops:
  0.0 43.6 %shard_map.55 = f32[16,1024]{1,0:T(8,128)} custom-call(bf16[4096,1024]{1,0:T(8,128)(2,1)} %psi_h.1, bf16[4096,128]{1,0:T(8,128)(2,1)} %trial_h.1, bf16[4096,1536]{1,0:T(8,128)(2,1)} %beta_h.1, f32[18,18,128]{2,1,0:T(8,128)} %bitcast.4, s32[1,128]{1,0:T(1,128)} %bitcast.5), custom_call_target="tpu_custom_call" | custom-call | tf_op jit(solution)/shard_map/pallas_call | solution.py:451
  43.6 1.5 %copy.7 = f32[1024,16]{0,1:T(8,128)} copy(f32[1024,16]{0,1:T(8,128)} %bitcast.3) | data formatting | bytes 131072

commit v6 on v5

--- a/solution.py
+++ b/solution.py
@@ -399,25 +399,29 @@
         f += jnp.dot(w_lo[...], g_hi[:, at], preferred_element_type=F32)
         return f + fin[..., at].reshape(2 * cols, pw)
 
-    def share(c, f):
-        near = routes[c % 3][0]
+    def share(c, _):
         at = aligned(c, pw)
-        code, scale = encode(f)
-        scale3[c] = scale
-        code3[..., at] = code.reshape(2, 2, 2, 2, r2, pw)
-        fin[..., at] = f.reshape(2, 2, 2, 2, r2, pw)
-        for d in peers:
-            send(
-                code3.at[pick(near, d) + (slice(None), at)], scale3.at[c],
-                in3.at[d, :, :, :, at], in3s.at[c, d], recv3.at[c], device(near, d),
-            )
-
-    with jax.named_scope("share"):
-        f = product(0)
-        for c in range(psi_chunks):
-            later = product(c + 1) if c + 1 < psi_chunks else None
-            share(c, f)
-            f = later
+        with jax.named_scope("share"):
+            f = product(c)
+            code, scale = encode(f)
+            scale3[c] = scale
+            code3[..., at] = code.reshape(2, 2, 2, 2, r2, pw)
+            fin[..., at] = f.reshape(2, 2, 2, 2, r2, pw)
+        for i in range(psi_chunks):
+            near = routes[i % 3][0]
+            now = pl.ds(i * pw, pw)
+
+            @pl.when(c == i)
+            def _():
+                for d in peers:
+                    send(
+                        code3.at[pick(near, d) + (slice(None), now)], scale3.at[i],
+                        in3.at[d, :, :, :, now], in3s.at[i, d], recv3.at[i], device(near, d),
+                    )
+
+        return 0
+
+    lax.fori_loop(0, psi_chunks, share, 0)
     for c in range(psi_chunks):
         with jax.named_scope(f"mid3_{c}"):
             middle3(c)

time: 45.3 us -> 44.9 us (level)
  no operation moved by 1% of the time
where the time goes in v6:
time: 44.9 us; the launch traced here: 44.8 us
  Pallas kernels  43.3 us (96%)
  local copies, waits for them, and re-layouts  1.47 us (3%)
    pallas_call x1, Pallas kernels, fused(): pl.pallas_call(functools.partial(kernel, n, maxp), out_shape=jax.ShapeDty...  43.3 us
    unnamed x1, local copies, waits for them, and re-layouts  1.47 us

profile of v6, /device:TPU:0, one launch (start us, length us, event | category | flops | bytes accessed | tf_op | source)
XLA Modules:
  0.0 44.8 jit_solution(8543606178634595747)
XLA Ops:
  0.0 43.3 %shard_map.55 = f32[16,1024]{1,0:T(8,128)} custom-call(bf16[4096,1024]{1,0:T(8,128)(2,1)} %psi_h.1, bf16[4096,128]{1,0:T(8,128)(2,1)} %trial_h.1, bf16[4096,1536]{1,0:T(8,128)(2,1)} %beta_h.1, f32[18,18,128]{2,1,0:T(8,128)} %bitcast.4, s32[1,128]{1,0:T(1,128)} %bitcast.5), custom_call_target="tpu_custom_call" | custom-call | tf_op jit(solution)/shard_map/pallas_call | solution.py:455
  43.3 1.5 %copy.7 = f32[1024,16]{0,1:T(8,128)} copy(f32[1024,16]{0,1:T(8,128)} %bitcast.3) | data formatting | bytes 131072

commit v7 on v6

--- a/solution.py
+++ b/solution.py
@@ -142,7 +142,7 @@
         for d in peers:
             send(
                 code1b.at[cell(late, d) + (slice(None), at)], scale1b.at[c],
-                end1.at[d, :, at], end1s.at[c, d], recv1b.at[c], device(late, d),
+                end1.at[d, :, at], end1s.at[c, d], recv1b, device(late, d),
             )
 
     with jax.named_scope("q_wait"):
@@ -282,19 +282,24 @@
 
     lax.fori_loop(0, psi_chunks, early, 0)
 
-    plane, line = routes[0]
-
-    def share_w(at, recv, to):
-        a, b = wall.at[at], walls.at[at]
-        send(a, b, a, b, recv, to)
-
-    def block(d):
-        return (band,) + cell(line, d) + cell(plane, 0)
+    tracks = [(c, pl.ds(c * bw, bw)) + routes[c % 3] for c in range(beta_chunks)]
+
+    def block(plane, line, e):
+        bits = {**toggled(plane, 0), **toggled(line, e)}
+        return (band,) + tuple(bits[p] for p in (3, 2, 1, 0))
+
+    def share_w(c, at, lanes, recv, to):
+        pieces = [wall.at[at + (slice(None), lanes)]]
+        if c == 0:
+            pieces.append(walls.at[at])
+        for a in pieces:
+            pltpu.make_async_remote_copy(
+                src_ref=a, dst_ref=a, send_sem=sent, recv_sem=recv, **to
+            ).start()
 
     def weigh():
         with jax.named_scope("wait_z1"):
-            for c in range(beta_chunks):
-                landed(late1, recv1b.at[c])
+            landed(beta_chunks * late1, recv1b)
 
         with jax.named_scope("q_apply"):
             pieces = []
@@ -314,26 +319,28 @@
             top = functools.reduce(jnp.maximum, [jnp.abs(t) for t in tiles])
             top = jnp.max(top, axis=0, keepdims=True)
             code, scale = encode(acc, jnp.concatenate([top] * len(tiles), axis=1))
-            wall[(band,) + pick((3, 2), 0)[:2] + pick((1, 0), 0)[2:]] = code
-            walls[(band,) + pick((3, 2), 0)[:2] + pick((1, 0), 0)[2:]] = scale[:, :128]
-        for d in peers:
-            share_w(block(0), recv2.at[d - 1], device(line, d))
-        for d in peers:
-            share_w(block(0), recv2b.at[0], device(plane, d))
+            home = block((1, 0), (3, 2), 0)
+            wall[home] = code
+            walls[home] = scale[:, :128]
+        for d in peers:
+            for c, lanes, plane, line in tracks:
+                share_w(c, block(plane, line, 0), lanes, recv2.at[d - 1], device(line, d))
+        for d in peers:
+            for c, lanes, plane, line in tracks:
+                share_w(c, block(plane, line, 0), lanes, recv2b.at[0], device(plane, d))
 
     def relay(e):
         landed(one, recv2.at[e - 1])
         for d in peers:
-            share_w(block(e), recv2b.at[e], device(plane, d))
+            for c, lanes, plane, line in tracks:
+                share_w(c, block(plane, line, e), lanes, recv2b.at[e], device(plane, d))
 
     def across(e):
         landed(3 * one, recv2b.at[e])
-        row = (band,) + cell(line, e)
-        a, b = wall.at[row], walls.at[row]
-        send(a, b, a, b, recv2c.at[e], partner)
-
-    def spread(b, e):
-        high, low = cell(line, e)
+        for c, lanes, plane, line in tracks:
+            share_w(c, (band,) + pick(line, e), lanes, recv2c, partner)
+
+    def spread(b, high, low):
         scale = jnp.concatenate([walls[b, high, low]] * (p_size // 128), axis=-1)
         values = decode(wall[b, high, low], scale)
         top, rest = split2(values.reshape(4 * r1, p_size))
@@ -344,11 +351,9 @@
     def late(u, _):
         for when, steps in (
             (1, (weigh,)),
-            (3, (functools.partial(relay, 1),)),
-            (4, (functools.partial(relay, 2),)),
-            (5, (functools.partial(relay, 3), functools.partial(across, 0))),
-            (6, (functools.partial(across, 1),)),
-            (7, (functools.partial(across, 2),)),
+            (4, tuple(functools.partial(relay, e) for e in (1, 2, 3))),
+            (5, (functools.partial(across, 0),)),
+            (7, (functools.partial(across, 1),)),
         ):
 
             @pl.when(u == when)
@@ -366,14 +371,15 @@
     lax.fori_loop(0, (beta_chunks - 1) * psi_chunks, late, 0)
 
     with jax.named_scope("ag_xy"):
+        across(2)
         across(3)
     with jax.named_scope("spread_own"):
-        for e in range(4):
-            spread(band, e)
+        for i in range(4):
+            spread(band, i // 2, i % 2)
     with jax.named_scope("across"):
-        for e in range(4):
-            landed(4 * one, recv2c.at[e])
-            spread(1 - band, e)
+        landed(16 * one, recv2c)
+        for i in range(4):
+            spread(1 - band, i // 2, i % 2)
 
     def middle3(c):
         near, late = routes[c % 3]
@@ -503,10 +509,10 @@
             dma,
             dma,
             dma((bc,)),
-            dma((bc,)),
+            dma,
             dma((3,)),
             dma((4,)),
-            dma((4,)),
+            dma,
             dma((pc,)),
             dma((pc,)),
         ],

time: 44.9 us -> 44.7 us (level)
  no operation moved by 1% of the time
where the time goes in v7:
time: 44.7 us; the launch traced here: 44.5 us
  Pallas kernels  43.1 us (96%)
  local copies, waits for them, and re-layouts  1.47 us (3%)
    pallas_call x1, Pallas kernels, fused(): pl.pallas_call(functools.partial(kernel, n, maxp), out_shape=jax.ShapeDty...  43.1 us
    unnamed x1, local copies, waits for them, and re-layouts  1.47 us

profile of v7, /device:TPU:0, one launch (start us, length us, event | category | flops | bytes accessed | tf_op | source)
XLA Modules:
  0.0 44.5 jit_solution(708538165936296426)
XLA Ops:
  0.0 43.1 %shard_map.55 = f32[16,1024]{1,0:T(8,128)} custom-call(bf16[4096,1024]{1,0:T(8,128)(2,1)} %psi_h.1, bf16[4096,128]{1,0:T(8,128)(2,1)} %trial_h.1, bf16[4096,1536]{1,0:T(8,128)(2,1)} %beta_h.1, f32[18,18,128]{2,1,0:T(8,128)} %bitcast.4, s32[1,128]{1,0:T(1,128)} %bitcast.5), custom_call_target="tpu_custom_call" | custom-call | tf_op jit(solution)/shard_map/pallas_call | solution.py:461
  43.1 1.5 %copy.7 = f32[1024,16]{0,1:T(8,128)} copy(f32[1024,16]{0,1:T(8,128)} %bitcast.3) | data formatting | bytes 131072

commit v8 on v7

--- a/solution.py
+++ b/solution.py
@@ -10,7 +10,7 @@
 MESH = pl.DeviceIdType.MESH
 precise = lax.Precision.HIGHEST
 F32, BF16, I16 = jnp.float32, jnp.bfloat16, jnp.int16
-LEVELS, TINY = 32767.0, 1e-30
+LEVELS, TINY = 32767.0, 4e-34
 
 
 def contract(left, right, precision=None):

time: 44.7 us -> 44.7 us (level)
  no operation moved by 1% of the time
where the time goes in v8:
time: 44.7 us; the launch traced here: 44.5 us
  Pallas kernels  43.1 us (96%)
  local copies, waits for them, and re-layouts  1.47 us (3%)
    pallas_call x1, Pallas kernels, fused(): pl.pallas_call(functools.partial(kernel, n, maxp), out_shape=jax.ShapeDty...  43.1 us
    unnamed x1, local copies, waits for them, and re-layouts  1.47 us

profile of v8, /device:TPU:0, one launch (start us, length us, event | category | flops | bytes accessed | tf_op | source)
XLA Modules:
  0.0 44.5 jit_solution(12681046951085086172)
XLA Ops:
  0.0 43.1 %shard_map.55 = f32[16,1024]{1,0:T(8,128)} custom-call(bf16[4096,1024]{1,0:T(8,128)(2,1)} %psi_h.1, bf16[4096,128]{1,0:T(8,128)(2,1)} %trial_h.1, bf16[4096,1536]{1,0:T(8,128)(2,1)} %beta_h.1, f32[18,18,128]{2,1,0:T(8,128)} %bitcast.4, s32[1,128]{1,0:T(1,128)} %bitcast.5), custom_call_target="tpu_custom_call" | custom-call | tf_op jit(solution)/shard_map/pallas_call | solution.py:461
  43.1 1.5 %copy.7 = f32[1024,16]{0,1:T(8,128)} copy(f32[1024,16]{0,1:T(8,128)} %bitcast.3) | data formatting | bytes 131072
